TPU v7x, 128 devices: a whole 4x4x4 slice. The times are simulated.
128 devices in a mesh: freq: 8 (over y, core), mesh: 16 (over z, x).
Axes of the slice: x: 4, y: 4, z: 4, core: 2. Of those that a mesh axis runs over, the one named last changes fastest.
Arguments:
- spectrum: float32 [2, 216, 65536], P(None, 'freq', 'mesh'), may hold values from -84 to 84
- time_weights: float32 [2, 432], P(None, 'freq'), may hold values from -0.875 to 0.875
- interp_weights: float32 [2048, 128, 128], P('mesh'), may hold values from -0.5 to 0.5
- group_block: int32 [2048], P('mesh'), may hold values from 0 to 511, as said below
- group_count: int32 [16], P('mesh'), may hold values from 64 to 128, as said below
- wave_state: float32 [8, 2, 1048576], P('freq', None, 'mesh'), may hold values from -6 to 6
- neighbors: int32 [4, 8192], P(None, 'mesh'), may hold values from 0 to 575, as said below
- coupling: float32 [4, 1048576], P(None, 'mesh'), may hold values from 0.02 to 0.2
Outputs:
- series: float32 [432, 65536], P('freq', 'mesh')
- new_state: float32 [8, 2, 1048576], P('freq', None, 'mesh')
Inputs may be any that keep to these rules, and one draw needn't show every extreme that they name: `group_block`: partition o owns blocks o * 32 to o * 32 + 31. Of one partition's 128 groups at most 8 name blocks of one owner, and each partition has an owner named by exactly 8 of its live groups. The live groups of partition m are its first group_count[m]; some partition has exactly 128. `neighbors`: for the cell row with local row index u, a value e names local row e - 32 of the row's own partition when it lies in 32 .. (69632) // 128 - 1, else a row of the neighbouring partition below or above; never the row itself.
All inputs are finite; a program needn't handle non-finite values.
Results may differ from a plain program's by a relative error of at most 0.0001.
Values sent between devices are 32-bit elements; how exact they have to be, the bound alone decides.
A program may use at most 64 MiB of HBM per device.

v0:
```python
import math

import jax
import jax.numpy as jnp
from jax import lax
from jax.sharding import Mesh
from jax.sharding import PartitionSpec as P

HB = 4096
FREQ = ("freq_0", "freq_1")


highest = lax.Precision.HIGHEST


def extended_2(block, sides, width):
    for axis, dim in sides:
        count = lax.axis_size(axis)
        forward = [(i, i + 1) for i in range(count - 1)]
        backward = [(target, source) for source, target in forward]
        low = lax.ppermute(
            lax.slice_in_dim(block, block.shape[dim] - width, None, axis=dim), axis, forward
        )
        high = lax.ppermute(lax.slice_in_dim(block, 0, width, axis=dim), axis, backward)
        block = jnp.concatenate([low, block, high], axis=dim)
    return block


def split_up(x, dim, peers):
    before, after = (x.shape[:dim], x.shape[dim + 1 :])
    return jnp.moveaxis(x.reshape(*before, peers, -1, *after), dim, 0)


def joined_along(parts, dim):
    lengths = list(parts.shape[1:])
    lengths[dim] *= parts.shape[0]
    return jnp.moveaxis(parts, 0, dim).reshape(lengths)


def moved_by_axis(parts, axes, turns):
    inside = parts.shape[1:]
    out = parts.reshape(*(lax.axis_size(a) for a in axes), *inside)
    for k in turns:
        out = lax.all_to_all(out, axes[k], k, k, tiled=True)
    return out.reshape(-1, *inside)


def exchange_by_axis(x, axes, turns, split_dim, concat_dim):
    parts = split_up(x, split_dim, lax.axis_size(axes))
    return joined_along(moved_by_axis(parts, axes, turns), concat_dim)


def rank_within(owner_of, alive, group_range):
    earlier = (
        (owner_of[..., :, None] == owner_of[..., None, :])
        & alive[..., :, None]
        & (group_range[:, None] < group_range[None, :])
    )
    return jnp.sum(earlier.astype(jnp.int32), axis=-2)


def build_fourier_basis(sample_times, angular_frequency, time_horizon):
    phase_angles = (sample_times[:, None] * angular_frequency[None, :] % time_horizon).astype(
        jnp.float32
    )
    angles = phase_angles * (2.0 * math.pi / time_horizon)
    scales = jnp.where(angular_frequency == 0, 1.0, 2.0).astype(jnp.float32) / time_horizon
    return jnp.concatenate([jnp.cos(angles) * scales, -jnp.sin(angles) * scales], axis=1)


def advance(previous, current, forcing, neighbors, coupling):
    row_count = neighbors.shape[1]
    lane_count = current.shape[0] // row_count
    cell_rows = current.reshape(row_count, lane_count)
    extended = extended_2(cell_rows, (("mesh", 0),), HB // lane_count)
    beside_all = jnp.take(extended, neighbors, axis=0).reshape(neighbors.shape[0], current.shape[0])
    spread = jnp.sum(coupling * (beside_all - current[None, :]), axis=0)
    return 2.0 * current - previous + spread + forcing


def local(
    spectrum,
    time_weights,
    interp_weights,
    group_block,
    group_count,
    wave_state,
    neighbors,
    coupling,
):
    local_freqs = spectrum.shape[1]
    points = spectrum.shape[2]
    freq_devices = lax.axis_size(FREQ)
    time_horizon = 2 * local_freqs * freq_devices
    columns = exchange_by_axis(spectrum, FREQ, (1, 0), 2, 1)
    all_freqs = columns.shape[1]
    basis_row_matrix = build_fourier_basis(
        lax.iota(jnp.int32, time_horizon), lax.iota(jnp.int32, all_freqs), time_horizon
    )
    whole_time = jnp.dot(
        basis_row_matrix,
        columns.reshape(2 * all_freqs, columns.shape[2]),
        precision=highest,
        preferred_element_type=jnp.float32,
    )
    series = lax.all_to_all(whole_time, FREQ, split_axis=0, concat_axis=1, tiled=True)
    groups = interp_weights.shape[0]
    block_width = interp_weights.shape[1]
    owners_count = lax.axis_size("mesh")
    capacity = max(2, groups // owners_count)
    per_owner = points // block_width
    slot_range = lax.iota(jnp.int32, capacity)
    group_range = lax.iota(jnp.int32, groups)
    owner_range = lax.iota(jnp.int32, owners_count)
    my_live = group_range < group_count[0]
    my_owner = group_block // per_owner
    my_rank = rank_within(my_owner, my_live, group_range)
    my_slot = jnp.where(my_live, my_owner * capacity + my_rank, 0)
    wanted = (
        my_live[None, None, :]
        & (my_owner[None, None, :] == owner_range[:, None, None])
        & (my_rank[None, None, :] == slot_range[None, :, None])
    )
    local_index = group_block[None, None, :] - owner_range[:, None, None] * per_owner
    request = jnp.sum(jnp.where(wanted, local_index + 1, 0), axis=2) - 1
    asked = lax.all_to_all(
        request.reshape(owners_count * capacity), "mesh", split_axis=0, concat_axis=0, tiled=True
    )
    slot_block = jnp.maximum(asked, 0).reshape(owners_count, capacity)
    slot_live = (asked >= 0).reshape(owners_count, capacity)
    flat_block = slot_block.reshape(owners_count * capacity)
    flat_live = slot_live.reshape(owners_count * capacity).astype(jnp.float32)
    live_mask = my_live.astype(jnp.float32)
    weighted = jnp.dot(time_weights, series, precision=highest, preferred_element_type=jnp.float32)
    blocks = weighted.reshape(2, per_owner, block_width)
    outgoing = jnp.take(blocks, flat_block, axis=1) * flat_live[None, :, None]
    picked = (
        jnp.take(
            lax.all_to_all(outgoing, "mesh", split_axis=1, concat_axis=1, tiled=True),
            my_slot,
            axis=1,
        )
        * live_mask[None, :, None]
    )
    forcing = jnp.einsum("rgp,gfp->rgf", picked, interp_weights, precision=highest)
    cell_count = wave_state.shape[2]
    forcing = forcing.reshape(2, groups * block_width)
    forcing = jnp.pad(forcing, ((0, 0), (0, cell_count - groups * block_width)))
    previous = wave_state[0, 0]
    current = wave_state[0, 1]
    stepped = advance(previous, current, forcing[0], neighbors, coupling)
    stepped_again = advance(current, stepped, forcing[1], neighbors, coupling)
    new_state = jnp.stack([stepped, stepped_again])[None]
    return (series, new_state)


def solution(mesh):
    torus = Mesh(mesh.devices.reshape(4, 2, mesh.shape["mesh"]), ("freq_0", "freq_1", "mesh"))
    in_specs = (
        P(None, FREQ, "mesh"),
        P(None, FREQ),
        P("mesh", None, None),
        P("mesh"),
        P("mesh"),
        P(FREQ, None, "mesh"),
        P(None, "mesh"),
        P(None, "mesh"),
    )
    out_specs = (P(FREQ, "mesh"), P(FREQ, None, "mesh"))
    return jax.shard_map(local, mesh=torus, in_specs=in_specs, out_specs=out_specs, check_vma=False)
```

profile of v0, /device:TPU:6, one launch (start us, length us, event | category | flops | bytes accessed | tf_op | source)
XLA Modules:
  0.0 122.8 jit_solution(13568961261415463164)
XLA Ops:
  0.7 0.9 fusion.33
  1.5 2.7 %collective-permute-start.1 = (f32[32,128]{1,0:T(8,128)S(1)}, f32[32,128]{1,0:T(8,128)S(1)}, u32[]{:S(2)}, u32[]{:S(2)}) collective-permute-start(f32[32,128]{1,0:T(8,128)S(1)} %bitcast.107), channel_id=1, source_target_pairs={{1,0},{2,1},{3,2},{4,3},{5,4},{6,5},{7,6},{8,7},{9,8},{10,9},{11,1... | collective-permute-start | bytes 49160 | tf_op jit(solution)/shard_map/ppermute | solution.py:24
  4.3 5.2 %collective-permute-start = (f32[32,128]{1,0:T(8,128)S(1)}, f32[32,128]{1,0:T(8,128)S(1)}, u32[]{:S(2)}, u32[]{:S(2)}) collective-permute-start(f32[32,128]{1,0:T(8,128)S(1)} %bitcast.106), channel_id=1, source_target_pairs={{0,1},{1,2},{2,3},{3,4},{4,5},{5,6},{6,7},{7,8},{8,9},{9,10},{10,1... | collective-permute-start | bytes 49160 | tf_op jit(solution)/shard_map/ppermute | solution.py:21
  9.5 1.5 %copy.58 = f32[27,1,8,2,512]{4,3,1,0,2:T(2,128)S(1)} copy(f32[27,1,8,2,512]{4,3,2,1,0:T(2,128)} %bitcast.104) | data formatting | bytes 1769472 | tf_op jit(solution)/shard_map/reshape | solution.py:31
  11.0 0.3 copy.41
  11.3 4.4 %all_to_all.37 = f32[4,2,2,27,512]{4,0,3,2,1:T(4,128)S(1)} all-to-all(f32[4,2,2,27,512]{4,0,3,2,1:T(4,128)S(1)} %copy.41), channel_id=1, replica_groups=mesh['freq_0'=4,'freq_1'=2,'mesh'=16] {'freq_1'}, dimensions={1} | all-to-all | bytes 1769472 | tf_op jit(solution)/shard_map/all_to_all | solution.py:44
  15.8 1.4 %copy.42 = f32[4,2,2,27,512]{4,2,3,1,0:T(2,128)} copy(f32[4,2,2,27,512]{4,0,3,2,1:T(4,128)S(1)} %all_to_all.37) | data formatting | bytes 1769472 | tf_op jit(solution)/shard_map/all_to_all | solution.py:44
  17.1 4.5 %all-to-all-start.1 = ((f32[4,2,2,27,512]{4,2,3,1,0:T(2,128)}), f32[4,2,2,27,512]{4,2,3,1,0:T(2,128)S(1)}, u32[]{:S(2)}, u32[]{:S(2)}) async-start(f32[4,2,2,27,512]{4,2,3,1,0:T(2,128)} %copy.42), calls=%async_computation.1 | async-start | bytes 1769472 | tf_op jit(solution)/shard_map/all_to_all | solution.py:44
  22.3 0.1 convert_reduce_fusion
  22.5 1.1 fusion.32
  23.6 0.1 subtract_add_fusion
  23.7 0.4 select_reduce_fusion
  24.1 0.7 copy.46
  24.8 2.0 %cosine_multiply_fusion = (f32[8,54,216]{2,1,0:T(8,128)S(1)}, f32[8,54,216]{2,1,0:T(8,128)S(1)}) fusion(f32[216]{0:T(256)S(1)} %fusion.28, s32[8,54]{1,0:T(8,128)S(1)} %multiply_add_fusion), kind=kLoop, calls=%fused_computation.27 | loop fusion | flops 1119744 | bytes 749088 | tf_op jit(solution)/shard_map/mul | solution.py:68
  26.9 8.4 %all-to-all-done.1 = f32[4,2,2,27,512]{4,2,3,1,0:T(2,128)S(1)} async-done(((f32[4,2,2,27,512]{4,2,3,1,0:T(2,128)}), f32[4,2,2,27,512]{4,2,3,1,0:T(2,128)S(1)}, u32[]{:S(2)}, u32[]{:S(2)}) %all-to-all-start.1) | async-done | bytes 884768 | tf_op jit(solution)/shard_map/all_to_all | solution.py:44
  35.2 7.8 %all-to-all-start.3 = ((s32[16,8,1]{1,2,0:T(1,128)}), s32[16,8,1]{1,2,0:T(1,128)S(1)}, u32[]{:S(2)}, u32[]{:S(2)}) async-start(s32[16,8,1]{1,2,0:T(1,128)} %copy.46), calls=%async_computation.3 | async-start | bytes 16384 | tf_op jit(solution)/shard_map/all_to_all | solution.py:126
  43.1 0.2 copy.57
  43.3 0.1 reshape.338
  43.4 2.6 %fusion.4 = f32[8,54,512]{2,1,0:T(8,128)} fusion(f32[432,512,1]{1,0,2:T(8,128)S(1)} %reshape.338, f32[8,54,216]{2,1,0:T(8,128)S(1)} %get-tuple-element.14, f32[8,54,216]{2,1,0:T(8,128)S(1)} %get-tuple-element.13), kind=kOutput, calls=%fused_computation.15 | convolution fusion | flops 1146804480 | bytes 2515968 | tf_op jit(solution)/shard_map/dot_general | solution.py:100
  46.0 2.5 %all-to-all-done.3 = s32[16,8,1]{1,2,0:T(1,128)S(1)} async-done(((s32[16,8,1]{1,2,0:T(1,128)}), s32[16,8,1]{1,2,0:T(1,128)S(1)}, u32[]{:S(2)}, u32[]{:S(2)}) %all-to-all-start.3) | async-done | bytes 544 | tf_op jit(solution)/shard_map/all_to_all | solution.py:126
  48.5 4.2 %all-to-all-start.2 = ((f32[8,54,512]{2,1,0:T(8,128)}), f32[8,54,512]{2,1,0:T(8,128)}, u32[]{:S(2)}, u32[]{:S(2)}) async-start(f32[8,54,512]{2,1,0:T(8,128)} %fusion.4), calls=%async_computation.2 | async-start | bytes 1835008 | tf_op jit(solution)/shard_map/all_to_all | solution.py:106
  52.8 0.1 reshape.310
  53.0 0.1 le.31
  53.1 0.1 reshape.291
  53.2 5.5 %gather_fusion.2 = f32[2048,128]{1,0:T(8,128)S(1)} fusion(f32[576,128]{1,0:T(8,128)S(1)} %pad_maximum_fusion, s32[2048]{0:T(1024)S(1)} %broadcast_clamp_fusion), kind=kCustom, calls=%fused_computation.clone | custom fusion | bytes 2105344 | tf_op jit(solution)/shard_map/jit(_take)/gather | solution.py:76
  58.7 0.3 select_bitcast_fusion.1
  59.1 8.3 %all-to-all-done.2 = f32[8,54,512]{2,1,0:T(8,128)} async-done(((f32[8,54,512]{2,1,0:T(8,128)}), f32[8,54,512]{2,1,0:T(8,128)}, u32[]{:S(2)}, u32[]{:S(2)}) %all-to-all-start.2) | async-done | bytes 884768 | tf_op jit(solution)/shard_map/all_to_all | solution.py:106
  67.3 1.7 %copy.44 = f32[54,8,512]{2,1,0:T(8,128)S(1)} copy(f32[54,8,512]{2,0,1:T(8,128)} %bitcast.4) | data formatting | bytes 1769472 | tf_op jit(solution)/shard_map/all_to_all | solution.py:106
  69.1 0.5 copy.49
  69.6 0.9 copy-done.2
  70.6 0.6 convolution_bitcast_fusion.1
  71.2 0.7 gather_fusion
  71.9 1.0 multiply_bitcast_fusion
  72.9 5.4 %all-to-all-start.4 = ((f32[2,128,128]{2,0,1:T(2,128)}), f32[2,128,128]{2,0,1:T(2,128)S(1)}, u32[]{:S(2)}, u32[]{:S(2)}) async-start(f32[2,128,128]{2,0,1:T(2,128)} %multiply_bitcast_fusion), calls=%async_computation.4 | async-start | bytes 262144 | tf_op jit(solution)/shard_map/all_to_all | solution.py:139
  78.3 1.4 %fusion.3 = f32[65536]{0:T(1024)S(1)} fusion(f32[4,65536]{1,0:T(4,128)S(1)} %copy-done.1, f32[1,4,512,128]{3,2,1,0:T(8,128)S(1)} %select_bitcast_fusion.1, f32[65536]{0:T(1024)S(1)} %bitcast.89), kind=kLoop, calls=%fused_computation.11 | loop fusion | flops 720896 | bytes 2621440 | tf_op jit(solution)/shard_map/reduce_sum | solution.py:77
  79.8 4.4 %all-to-all-done.4 = f32[2,128,128]{2,0,1:T(2,128)S(1)} async-done(((f32[2,128,128]{2,0,1:T(2,128)}), f32[2,128,128]{2,0,1:T(2,128)S(1)}, u32[]{:S(2)}, u32[]{:S(2)}) %all-to-all-start.4) | async-done | bytes 131104 | tf_op jit(solution)/shard_map/all_to_all | solution.py:139
  84.1 0.7 gather_fusion.1
  84.9 15.5 %convolution_bitcast_fusion = f32[2,16384]{1,0:T(2,128)S(1)} fusion(f32[128,128,128]{2,1,0:T(8,128)} %param.12, f32[128,2,128]{2,1,0:T(2,128)S(1)} %gather_fusion.1, pred[128]{0:T(512)(128)(4,1)S(1)} %get-tuple-element.3, f32[128]{0:T(128)S(1)} %get-tuple-element.15), kind=kOutput, calls=%fused_computation.4 | convolution fusion | flops 50397184 | bytes 8651392 | tf_op jit(solution)/shard_map/rgp,gfp->rgf/dot_general | solution.py:145
  100.4 0.6 fusion.16
  100.9 1.0 fusion.14
  102.0 3.9 %collective-permute-start.2 = (f32[32,128]{1,0:T(8,128)S(1)}, f32[32,128]{1,0:T(8,128)S(1)}, u32[]{:S(2)}, u32[]{:S(2)}) collective-permute-start(f32[32,128]{1,0:T(8,128)S(1)} %get-tuple-element.9), channel_id=1, source_target_pairs={{0,1},{1,2},{2,3},{3,4},{4,5},{5,6},{6,7},{7,8},{8,9},{9,10},{10,1... | collective-permute-start | bytes 49160 | tf_op jit(solution)/shard_map/ppermute | solution.py:21
  105.9 1.9 %collective-permute-start.3 = (f32[32,128]{1,0:T(8,128)S(1)}, f32[32,128]{1,0:T(8,128)S(1)}, u32[]{:S(2)}, u32[]{:S(2)}) collective-permute-start(f32[32,128]{1,0:T(8,128)S(1)} %get-tuple-element.10), channel_id=1, source_target_pairs={{1,0},{2,1},{3,2},{4,3},{5,4},{6,5},{7,6},{8,7},{9,8},{10,9},{11,1... | collective-permute-start | bytes 49160 | tf_op jit(solution)/shard_map/ppermute | solution.py:24
  107.8 5.8 %collective-permute-done.3 = f32[32,128]{1,0:T(8,128)S(1)} collective-permute-done((f32[32,128]{1,0:T(8,128)S(1)}, f32[32,128]{1,0:T(8,128)S(1)}, u32[]{:S(2)}, u32[]{:S(2)}) %collective-permute-start.3) | collective-permute-done | bytes 16416 | tf_op jit(solution)/shard_map/ppermute | solution.py:24
  113.7 5.5 %gather_fusion.3 = f32[2048,128]{1,0:T(8,128)S(1)} fusion(f32[576,128]{1,0:T(8,128)S(1)} %pad_maximum_fusion.1, s32[2048]{0:T(1024)S(1)} %broadcast_clamp_fusion), kind=kCustom, calls=%fused_computation.1.clone | custom fusion | bytes 2105344 | tf_op jit(solution)/shard_map/jit(_take)/gather | solution.py:76
  119.1 0.3 select_bitcast_fusion
  119.5 1.5 %fusion.1 = f32[65536]{0:T(1024)S(1)} fusion(f32[4,65536]{1,0:T(4,128)S(1)} %copy-done.1, f32[1,4,512,128]{3,2,1,0:T(8,128)S(1)} %select_bitcast_fusion, f32[65536]{0:T(1024)S(1)} %bitcast.92), kind=kLoop, calls=%fused_computation.8 | loop fusion | flops 720896 | bytes 2621440 | tf_op jit(solution)/shard_map/reduce_sum | solution.py:77
  121.0 0.6 fusion.13
  121.6 1.3 %maximum_bitcast_fusion = f32[1,2,65536]{2,1,0:T(2,128)} fusion(f32[1,65536]{1,0:T(1,128)S(1)} %fusion.13, f32[1,65536]{1,0:T(1,128)S(1)} %get-tuple-element.11), kind=kLoop, calls=%fused_computation.23 | loop fusion | flops 131072 | bytes 1048576 | tf_op jit(solution)/shard_map/broadcast_in_dim | solution.py:153
  (43 shorter events, 0.4 us)
Async XLA Ops:
  0.6 69.9 %copy-start = (f32[2,54]{1,0:T(2,128)S(1)}, f32[2,54]{1,0:T(2,128)}, u32[]{:S(2)}) copy-start(f32[2,54]{1,0:T(2,128)} %param.11) | copy-start | bytes 1300
  0.6 21.8 %copy-start.3 = (f32[1,2,65536]{2,1,0:T(2,128)S(1)}, f32[1,2,65536]{2,1,0:T(2,128)}, u32[]{:S(2)}) copy-start(f32[1,2,65536]{2,1,0:T(2,128)} %param.15) | copy-start | bytes 1572868
  0.7 21.6 %copy-start.8 = (s32[128]{0:T(128)S(1)}, s32[128]{0:T(128)}, u32[]{:S(2)}) copy-start(s32[128]{0:T(128)} %param.13) | copy-start | bytes 1540
  0.7 24.1 %copy-start.7 = (s32[4,512]{1,0:T(4,128)S(1)}, s32[4,512]{1,0:T(4,128)}, u32[]{:S(2)}) copy-start(s32[4,512]{1,0:T(4,128)} %param.16) | copy-start | bytes 24580
  1.5 51.6 %collective-permute-start.1 = (f32[32,128]{1,0:T(8,128)S(1)}, f32[32,128]{1,0:T(8,128)S(1)}, u32[]{:S(2)}, u32[]{:S(2)}) collective-permute-start(f32[32,128]{1,0:T(8,128)S(1)} %bitcast.107), channel_id=1, source_target_pairs={{1,0},{2,1},{3,2},{4,3},{5,4},{6,5},{7,6},{8,7},{9,8},{10,9},{11,1... | collective-permute-start | bytes 49160 | tf_op jit(solution)/shard_map/ppermute | solution.py:24
  4.3 48.9 %collective-permute-start = (f32[32,128]{1,0:T(8,128)S(1)}, f32[32,128]{1,0:T(8,128)S(1)}, u32[]{:S(2)}, u32[]{:S(2)}) collective-permute-start(f32[32,128]{1,0:T(8,128)S(1)} %bitcast.106), channel_id=1, source_target_pairs={{0,1},{1,2},{2,3},{3,4},{4,5},{5,6},{6,7},{7,8},{8,9},{9,10},{10,1... | collective-permute-start | bytes 49160 | tf_op jit(solution)/shard_map/ppermute | solution.py:21
  17.1 18.1 %all-to-all-start.1 = ((f32[4,2,2,27,512]{4,2,3,1,0:T(2,128)}), f32[4,2,2,27,512]{4,2,3,1,0:T(2,128)S(1)}, u32[]{:S(2)}, u32[]{:S(2)}) async-start(f32[4,2,2,27,512]{4,2,3,1,0:T(2,128)} %copy.42), calls=%async_computation.1 | async-start | bytes 1769472 | tf_op jit(solution)/shard_map/all_to_all | solution.py:44
  35.2 13.3 %all-to-all-start.3 = ((s32[16,8,1]{1,2,0:T(1,128)}), s32[16,8,1]{1,2,0:T(1,128)S(1)}, u32[]{:S(2)}, u32[]{:S(2)}) async-start(s32[16,8,1]{1,2,0:T(1,128)} %copy.46), calls=%async_computation.3 | async-start | bytes 16384 | tf_op jit(solution)/shard_map/all_to_all | solution.py:126
  48.5 18.8 %all-to-all-start.2 = ((f32[8,54,512]{2,1,0:T(8,128)}), f32[8,54,512]{2,1,0:T(8,128)}, u32[]{:S(2)}, u32[]{:S(2)}) async-start(f32[8,54,512]{2,1,0:T(8,128)} %fusion.4), calls=%async_computation.2 | async-start | bytes 1835008 | tf_op jit(solution)/shard_map/all_to_all | solution.py:106
  53.2 25.1 %copy-start.1 = (f32[4,65536]{1,0:T(4,128)S(1)}, f32[4,65536]{1,0:T(4,128)}, u32[]{:S(2)}) copy-start(f32[4,65536]{1,0:T(4,128)} %param.17) | copy-start | bytes 3145732
  69.0 31.3 %copy-start.4 = (f32[1,2,65536]{2,1,0:T(2,128)S(1)}, f32[1,2,65536]{2,1,0:T(2,128)}, u32[]{:S(2)}) copy-start(f32[1,2,65536]{2,1,0:T(2,128)} %param.15) | copy-start | bytes 1572868
  69.6 0.9 copy-start.2
  72.9 11.2 %all-to-all-start.4 = ((f32[2,128,128]{2,0,1:T(2,128)}), f32[2,128,128]{2,0,1:T(2,128)S(1)}, u32[]{:S(2)}, u32[]{:S(2)}) async-start(f32[2,128,128]{2,0,1:T(2,128)} %multiply_bitcast_fusion), calls=%async_computation.4 | async-start | bytes 262144 | tf_op jit(solution)/shard_map/all_to_all | solution.py:139
  100.4 7.5 %copy-start.5 = (f32[2,16384]{1,0:T(2,128)}, f32[2,16384]{1,0:T(2,128)S(1)}, u32[]{:S(2)}) copy-start(f32[2,16384]{1,0:T(2,128)S(1)} %convolution_bitcast_fusion) | copy-start | bytes 393220
  102.0 5.9 %collective-permute-start.2 = (f32[32,128]{1,0:T(8,128)S(1)}, f32[32,128]{1,0:T(8,128)S(1)}, u32[]{:S(2)}, u32[]{:S(2)}) collective-permute-start(f32[32,128]{1,0:T(8,128)S(1)} %get-tuple-element.9), channel_id=1, source_target_pairs={{0,1},{1,2},{2,3},{3,4},{4,5},{5,6},{6,7},{7,8},{8,9},{9,10},{10,1... | collective-permute-start | bytes 49160 | tf_op jit(solution)/shard_map/ppermute | solution.py:21
  105.9 7.7 %collective-permute-start.3 = (f32[32,128]{1,0:T(8,128)S(1)}, f32[32,128]{1,0:T(8,128)S(1)}, u32[]{:S(2)}, u32[]{:S(2)}) collective-permute-start(f32[32,128]{1,0:T(8,128)S(1)} %get-tuple-element.10), channel_id=1, source_target_pairs={{1,0},{2,1},{3,2},{4,3},{5,4},{6,5},{7,6},{8,7},{9,8},{10,9},{11,1... | collective-permute-start | bytes 49160 | tf_op jit(solution)/shard_map/ppermute | solution.py:24
  113.6 7.3 %copy-start.6 = (f32[2,16384]{1,0:T(2,128)S(1)}, f32[2,16384]{1,0:T(2,128)}, u32[]{:S(2)}) copy-start(f32[2,16384]{1,0:T(2,128)} %copy-done.5) | copy-start | bytes 393220
where the time goes:
time: 123 us
  starting transfers between devices  35.7 us (29%)
  waiting for transfers between devices  29.4 us (24%)
  local copies, waits for them, and re-layouts  22.1 us (18%)
  matrix products  18.7 us (15%)
  other arithmetic  10.8 us (9%)
  blocking collectives  4.43 us (4%)
  between operations  1.67 us (1%)
    dot_general x1, matrix products, local(): jnp.einsum('rgp,gfp->rgf', picked, interp_weights, precision=highest)  15.5 us
    gather x2, local copies, waits for them, and re-layouts, advance(): jnp.take(extended, neighbors, axis=0)  10.9 us
    ppermute x2, starting transfers between devices, extended_2(): lax.ppermute(lax.slice_in_dim(block, block.shape[dim] - width, None, axis...  9.14 us
    all_to_all x1, waiting for transfers between devices, moved_by_axis(): out = lax.all_to_all(out, axes[k], k, k, tiled=True)  8.39 us
    all_to_all x1, waiting for transfers between devices, local(): lax.all_to_all(whole_time, FREQ, split_axis=0, concat_axis=1, tiled=True)  8.25 us
    all_to_all x1, starting transfers between devices, local(): lax.all_to_all(request.reshape(owners_count * capacity), 'mesh', split_ax...  7.84 us
    ppermute x2, waiting for transfers between devices, extended_2(): lax.ppermute(lax.slice_in_dim(block, 0, width, axis=dim), axis, backward)  5.8 us
    all_to_all x1, starting transfers between devices, local(): lax.all_to_all(outgoing, 'mesh', split_axis=1, concat_axis=1, tiled=True)  5.38 us
  transfers between devices with their start and end apart: 8, of which 5 were waited for; matrix products, arithmetic and copies ran while one was open for 15% of the time, Pallas kernels for 0%

commit v1 on v0

v1 whole, which is shorter than its diff:
```python
import math

import jax
import jax.numpy as jnp
import numpy as np
from jax import lax
from jax.experimental import pallas as pl
from jax.experimental.pallas import tpu as pltpu
from jax.sharding import PartitionSpec as P

MESH = pl.DeviceIdType.MESH
F32 = jnp.float32
BF16 = jnp.bfloat16

NF = 216
NT = 432
FD = 8
MD = 16
FL = NF // FD
TL = NT // FD
KP = 56
NP = 4096
COLS = NP // FD
HALVES = 2
HC = COLS // HALVES
BLK = 128
NBLK = NP // BLK
GROUPS = 128
ROWS = 512
HALO = 32
EXT = 640


def split_bf16(x):
    hi = x.astype(BF16)
    lo = (x - hi.astype(F32)).astype(BF16)
    return hi, lo


def host_split(x):
    hi = np.asarray(x, np.float32).astype(jnp.bfloat16)
    lo = (x - hi.astype(np.float64)).astype(jnp.bfloat16)
    return hi, lo


def host_basis():
    t = np.arange(NT)[:, None]
    k = np.arange(NF)[None, :]
    angle = (t * k % NT) * (2.0 * math.pi / NT)
    scale = np.where(k == 0, 1.0, 2.0) / NT
    full = np.zeros((FD, KP, FD, KP))
    full[:, :TL, :, :FL] = (np.cos(angle) * scale).reshape(FD, TL, FD, FL)
    full[:, :TL, :, FL : 2 * FL] = (-np.sin(angle) * scale).reshape(FD, TL, FD, FL)
    basis = np.stack(host_split(full.reshape(FD * KP, FD * KP)))
    own = np.zeros((FD, 64, FD, 64))
    own[:, :KP, :, :KP] = full.transpose(2, 1, 0, 3)
    own = own.reshape(FD, 64, FD * 64)
    return basis, np.stack(host_split(own), axis=1)


def dot(a, b):
    return jnp.dot(a, b, preferred_element_type=F32)


def dot_t(a, b):
    return lax.dot_general(a, b, (((1,), (1,)), ((), ())), preferred_element_type=F32)


def kernel(
    spec_h, tw_h, w_h, gb_h, gc_h, ws_h, nb_h, cp_h, basis_h, own_h,
    series_o, state_o,
    xs, xp, tws, twr, twf, cb, basis, r, s2, pb, ra, wsum, ag, wf, whl, oh, ws, cp, nb, gb, gc,
    hs, hcur, hb1, hpush, hps, sb, base1, base2, ns, lh, ee,
    lsem, tw_s, tw_r, x_s, x_r, a_s, a_r, g_s, g_r, h_s, h_r, y_s, y_r, mesh_sem,
):
    f = lax.axis_index("freq")
    m = lax.axis_index("mesh")
    z, x = m // 4, m % 4

    def fdev(d):
        return (lax.rem(f + d, FD), m)

    def mdev(d):
        return (f, lax.rem(m + d, MD))

    def remote(src, dst, ssem, rsem, dev):
        return pltpu.make_async_remote_copy(
            src_ref=src, dst_ref=dst, send_sem=ssem, recv_sem=rsem, device_id=dev, device_id_type=MESH
        )

    bar = pltpu.get_barrier_semaphore()
    xline = [(f, z * 4 + lax.rem(x + d, 4)) for d in range(1, 4)]
    zline = [(f, lax.rem(z + d, 4) * 4 + x) for d in range(1, 4)]
    first = [fdev(d) for d in range(1, FD)] + xline + zline
    for dev in first:
        pl.semaphore_signal(bar, inc=1, device_id=dev, device_id_type=MESH)

    loads = [
        (spec_h, xs), (tw_h, tws), (own_h.at[f], cb), (nb_h, nb), (gb_h, gb), (gc_h, gc),
        (ws_h, ws), (cp_h, cp), (basis_h, basis), (w_h, wf),
    ]
    local = [pltpu.make_async_copy(s, d, lsem.at[i]) for i, (s, d) in enumerate(loads)]
    for c in local:
        c.start()

    twf[...] = jnp.zeros_like(twf)
    xp[KP - 8 :, :] = jnp.zeros((8, NP), F32)
    sb[ROWS:, :] = jnp.zeros((EXT - ROWS, 256), BF16)
    local[0].wait()
    xp[0:FL, :] = xs[0]
    xp[FL : 2 * FL, :] = xs[1]
    local[1].wait()
    local[6].wait()
    hs[0] = ws[pl.ds(1, HALO, stride=2), :]
    hs[1] = ws[pl.ds(2 * (ROWS - HALO) + 1, HALO, stride=2), :]

    pl.semaphore_wait(bar, len(first))

    tw_c = [remote(tws, twr.at[f], tw_s.at[d], tw_r.at[d], fdev(d)) for d in range(1, FD)]
    for c in tw_c:
        c.start()

    def x_copy(h, d):
        to = lax.rem(f + d, FD)
        cols = pl.ds(pl.multiple_of(to * COLS + h * HC, 128), HC)
        rows = pl.ds(pl.multiple_of(f * KP, 8), KP)
        return remote(xp.at[:, cols], r.at[h, rows], x_s.at[h, d], x_r.at[h, d], (to, m))

    x_c = [[x_copy(h, d) for d in range(1, FD)] for h in range(HALVES)]
    for c in x_c[0]:
        c.start()
    for dev in xline:
        pl.semaphore_signal(mesh_sem, inc=1, device_id=dev, device_id_type=MESH)
    own_x = [
        pltpu.make_async_copy(
            xp.at[:, pl.ds(pl.multiple_of(f * COLS + h * HC, 128), HC)],
            r.at[h, pl.ds(pl.multiple_of(f * KP, 8), KP)],
            lsem.at[10 + h],
        )
        for h in range(HALVES)
    ]
    for c in own_x:
        c.start()

    local[2].wait()
    for c in tw_c:
        c.wait_recv()
    twr[f] = tws[...]
    for w in range(FD):
        twf[2 * w : 2 * w + 2, 0:TL] = twr[w]
    th, tl = split_bf16(twf[:, 0:64])
    g_all = dot(th, cb[0]) + dot(tl, cb[0]) + dot(th, cb[1])
    row_w = lax.broadcasted_iota(jnp.int32, (16, 128), 0) // 2
    lane_w = lax.broadcasted_iota(jnp.int32, (16, 128), 1) // 64
    g2 = jnp.zeros((16, 128), F32)
    for i in range(4):
        g2 = g2 + jnp.where(lane_w + 2 * i == row_w, g_all[:, 128 * i : 128 * (i + 1)], 0.0)
    g = (g2 + pltpu.roll(g2, 64, 1))[:, 0:KP]
    gh, gl = split_bf16(g)
    ghl = jnp.concatenate([gh, gl], axis=0)
    for q in range(8):
        xh, xl = split_bf16(xp[:, 512 * q : 512 * (q + 1)])
        both = dot(ghl, xh)
        part = both[0:16] + both[16:32] + dot(gh, xl)
        for b in range(4):
            pb[pl.ds(4 * q + b, 16, stride=NBLK), :] = part[:, 128 * b : 128 * (b + 1)]

    def a_copy(d):
        to = lax.rem(f + d, FD)
        return remote(pb.at[pl.ds(pl.multiple_of(to * 64, 8), 64)], ra.at[f], a_s.at[d], a_r.at[d], (to, m))

    a_c = [a_copy(d) for d in range(1, FD)]
    for c in a_c:
        c.start()
    for c in x_c[1]:
        c.start()
    ra[f] = pb[pl.ds(pl.multiple_of(f * 64, 8), 64), :]

    pl.semaphore_wait(mesh_sem, 3)
    up, down = mdev(1), mdev(MD - 1)

    def halo_pair(i, low_src, high_src, dst):
        return [
            remote(low_src, dst.at[1], h_s.at[i], h_r.at[i], down),
            remote(high_src, dst.at[0], h_s.at[i + 1], h_r.at[i + 1], up),
        ]

    cur_c = halo_pair(0, hs.at[0], hs.at[1], hcur)
    for c in cur_c:
        c.start()

    local[3].wait()
    nbv = nb[...]
    nbv = jnp.where(nbv >= ROWS + HALO, nbv, jnp.where(nbv < HALO, nbv + ROWS, nbv - HALO)).astype(F32)
    lane = lax.broadcasted_iota(jnp.int32, (128, 128), 1).astype(F32)
    for n in range(4):
        for ut in range(4):
            col = jnp.transpose(jnp.broadcast_to(nbv[n : n + 1, 128 * ut : 128 * (ut + 1)], (128, 128)))
            for kt in range(EXT // 128):
                hot = jnp.where(col == lane + float(128 * kt), 1.0, 0.0).astype(BF16)
                oh[ut, 128 * n : 128 * (n + 1), 128 * kt : 128 * (kt + 1)] = hot

    local[9].wait()

    def split_w(i, carry):
        rows = pl.ds(pl.multiple_of(i * 512, 512), 512)
        hi, lo = split_bf16(wf[rows, :])
        whl[rows, 0:128] = hi
        whl[rows, 128:256] = lo
        return carry

    lax.fori_loop(0, GROUPS * BLK // 512, split_w, 0)

    for i in (7,):
        local[i].wait()

    def put_ext(lo_row, value):
        hi, lo = split_bf16(value)
        sb[lo_row : lo_row + value.shape[0], 0:128] = hi
        sb[lo_row : lo_row + value.shape[0], 128:256] = lo

    def put_halo(buf):
        put_ext(ROWS, jnp.where(m > 0, buf[0], 0.0))
        put_ext(ROWS + HALO, jnp.where(m < MD - 1, buf[1], 0.0))

    def spread(ut, v):
        e = dot(oh[ut], sb[...])
        total = jnp.zeros((128, 128), F32)
        for n in range(4):
            c = cp[pl.ds(512 * ut + n, 128, stride=4), :]
            total = total + c * (e[128 * n : 128 * (n + 1), 0:128] + e[128 * n : 128 * (n + 1), 128:256] - v)
        return total

    put_ext(0, ws[pl.ds(1, ROWS, stride=2), :])
    for c in cur_c:
        c.wait_recv()
    put_halo(hcur)
    for ut in range(4):
        cur = ws[pl.ds(256 * ut + 1, 128, stride=2), :]
        prev = ws[pl.ds(256 * ut, 128, stride=2), :]
        base1[128 * ut : 128 * (ut + 1), :] = 2.0 * cur - prev + spread(ut, cur)
    b1_c = halo_pair(2, base1.at[0:HALO], base1.at[ROWS - HALO : ROWS], hb1)
    for c in b1_c:
        c.start()

    local[8].wait()

    def y_copy(h, d):
        to = lax.rem(f + d, FD)
        cols = pl.ds(pl.multiple_of(f * COLS + h * HC, 128), HC)
        return remote(s2.at[h, to], series_o.at[:, cols], y_s.at[h, d], y_r.at[h, d], (to, m))

    y_c = [[y_copy(h, d) for d in range(1, FD)] for h in range(HALVES)]
    own_y = []

    def transform(h):
        for c in x_c[h]:
            c.wait_recv()
        own_x[h].wait()
        xh, xl = split_bf16(r[h])
        out = dot(basis[0], xh) + dot(basis[0], xl) + dot(basis[1], xh)
        for w in range(FD):
            s2[h, w] = out[KP * w : KP * w + TL]
        for c in y_c[h]:
            c.start()
        c = pltpu.make_async_copy(
            s2.at[h, f], series_o.at[:, pl.ds(pl.multiple_of(f * COLS + h * HC, 128), HC)], lsem.at[12 + h]
        )
        c.start()
        own_y.append(c)

    transform(0)

    for c in a_c:
        c.wait_recv()
    total = ra[0]
    for i in range(1, FD):
        total = total + ra[i]
    wsum[...] = total
    ag[m] = total
    g_c = [remote(wsum, ag.at[m], g_s.at[d], g_r.at[d], mdev(d)) for d in range(1, MD)]
    for c in g_c:
        c.start()

    put_ext(0, base1[...])
    for c in b1_c:
        c.wait_recv()
    put_halo(hb1)
    for ut in range(4):
        cur = ws[pl.ds(256 * ut + 1, 128, stride=2), :]
        b1 = base1[128 * ut : 128 * (ut + 1), :]
        base2[128 * ut : 128 * (ut + 1), :] = 2.0 * b1 - cur + spread(ut, b1)

    transform(1)

    local[4].wait()
    local[5].wait()
    gbv = gb[...].astype(F32)
    index = lax.broadcasted_iota(jnp.int32, (1, 128), 1)
    gbv = jnp.where(index < gc[...], gbv, -1.0)
    gcol = jnp.transpose(jnp.broadcast_to(gbv, (128, 128)))
    pick = jnp.concatenate(
        [jnp.where(gcol == lane + float(128 * kt), 1.0, 0.0).astype(BF16) for kt in range(4)], axis=1
    )
    for c in g_c:
        c.wait_recv()
    for s in range(2):
        blocks = ag[:, NBLK * s : NBLK * (s + 1), :].reshape(MD * NBLK, BLK)
        hi, lo = split_bf16(blocks)
        ph = dot(pick, hi)
        lh[0, pl.ds(2 * s, 128, stride=4), :] = ph
        lh[1, pl.ds(2 * s, 128, stride=4), :] = ph
        lh[0, pl.ds(2 * s + 1, 128, stride=4), :] = dot(pick, lo)
        lh[1, pl.ds(2 * s + 1, 128, stride=4), :] = jnp.zeros((128, 128), F32)
    upper = lax.broadcasted_iota(jnp.int32, (8, 128), 0) < 4

    def interp(i, carry):
        for j in range(4):
            rows = pl.ds(pl.multiple_of(i * 32 + 8 * j, 8), 8)
            w = whl[pl.ds(pl.multiple_of(i * 1024 + 256 * j, 256), 256), :]
            left = jnp.concatenate([lh[0, rows, :], lh[1, rows, :]], axis=1).astype(BF16)
            out = dot_t(left, w)
            ee[rows, :] = jnp.where(upper, out[:, 0:128], out[:, 128:256])
        return carry

    lax.fori_loop(0, GROUPS // 8, interp, 0)
    push0 = ee[pl.ds(0, 128, stride=4), :] + ee[pl.ds(1, 128, stride=4), :]
    push1 = ee[pl.ds(2, 128, stride=4), :] + ee[pl.ds(3, 128, stride=4), :]
    hps[...] = push0[0:HALO]
    p_c = remote(hps, hpush, h_s.at[4], h_r.at[4], down)
    p_c.start()

    sb[ROWS : ROWS + HALO, :] = jnp.zeros((HALO, 256), BF16)
    put_ext(0, push0)
    p_c.wait_recv()
    put_ext(ROWS + HALO, jnp.where(m < MD - 1, hpush[...], 0.0))
    for ut in range(4):
        e = dot(oh[ut, :, 0:128], sb[0:128, :]) + dot(oh[ut, :, ROWS:EXT], sb[ROWS:EXT, :])
        total = jnp.zeros((128, 128), F32)
        for n in range(4):
            c = cp[pl.ds(512 * ut + n, 128, stride=4), :]
            en = e[128 * n : 128 * (n + 1), 0:128] + e[128 * n : 128 * (n + 1), 128:256]
            total = total + c * (en - push0 if ut == 0 else en)
        n1 = base1[128 * ut : 128 * (ut + 1), :]
        n2 = base2[128 * ut : 128 * (ut + 1), :] + total
        if ut == 0:
            n1 = n1 + push0
            n2 = n2 + 2.0 * push0 + push1
        ns[pl.ds(256 * ut, 128, stride=2), :] = n1
        ns[pl.ds(256 * ut + 1, 128, stride=2), :] = n2
    out_c = pltpu.make_async_copy(ns, state_o, lsem.at[14])
    out_c.start()

    for c in tw_c + x_c[0] + x_c[1] + a_c + g_c + cur_c + b1_c + [p_c] + y_c[0] + y_c[1]:
        c.wait_send()
    for c in y_c[0] + y_c[1]:
        c.wait_recv()
    for c in own_y:
        c.wait()
    out_c.wait()


def local_step(spectrum, time_weights, interp_weights, group_block, group_count, wave_state, neighbors, coupling):
    basis, own = host_basis()
    ws = wave_state.reshape(2, ROWS, 128).transpose(1, 0, 2).reshape(2 * ROWS, 128)
    cp = coupling.reshape(4, ROWS, 128).transpose(1, 0, 2).reshape(4 * ROWS, 128)
    any_spec = pl.BlockSpec(memory_space=pl.ANY)
    sem = pltpu.SemaphoreType.DMA
    series, state = pl.pallas_call(
        kernel,
        out_shape=(
            jax.ShapeDtypeStruct((TL, NP), F32),
            jax.ShapeDtypeStruct((2 * ROWS, 128), F32),
        ),
        in_specs=[any_spec] * 10,
        out_specs=(any_spec, any_spec),
        scratch_shapes=[
            pltpu.VMEM((2, FL, NP), F32),
            pltpu.VMEM((KP, NP), F32),
            pltpu.VMEM((2, TL), F32),
            pltpu.VMEM((FD, 2, TL), F32),
            pltpu.VMEM((16, 128), F32),
            pltpu.VMEM((2, 64, FD * 64), BF16),
            pltpu.VMEM((2, FD * KP, FD * KP), BF16),
            pltpu.VMEM((HALVES, FD * KP, HC), F32),
            pltpu.VMEM((HALVES, FD, TL, HC), F32),
            pltpu.VMEM((16 * NBLK, BLK), F32),
            pltpu.VMEM((FD, 64, BLK), F32),
            pltpu.VMEM((64, BLK), F32),
            pltpu.VMEM((MD, 64, BLK), F32),
            pltpu.VMEM((GROUPS * BLK, BLK), F32),
            pltpu.VMEM((GROUPS * BLK, 2 * BLK), BF16),
            pltpu.VMEM((4, 512, EXT), BF16),
            pltpu.VMEM((2 * ROWS, 128), F32),
            pltpu.VMEM((4 * ROWS, 128), F32),
            pltpu.VMEM((4, ROWS), jnp.int32),
            pltpu.VMEM((1, 128), jnp.int32),
            pltpu.VMEM((1, 1), jnp.int32),
            pltpu.VMEM((2, HALO, 128), F32),
            pltpu.VMEM((2, HALO, 128), F32),
            pltpu.VMEM((2, HALO, 128), F32),
            pltpu.VMEM((HALO, 128), F32),
            pltpu.VMEM((HALO, 128), F32),
            pltpu.VMEM((EXT, 256), BF16),
            pltpu.VMEM((ROWS, 128), F32),
            pltpu.VMEM((ROWS, 128), F32),
            pltpu.VMEM((2 * ROWS, 128), F32),
            pltpu.VMEM((2, 4 * GROUPS, BLK), F32),
            pltpu.VMEM((4 * GROUPS, BLK), F32),
            sem((16,)),
            sem((FD,)), sem((FD,)),
            sem((HALVES, FD)), sem((HALVES, FD)),
            sem((FD,)), sem((FD,)),
            sem((MD,)), sem((MD,)),
            sem((6,)), sem((6,)),
            sem((HALVES, FD)), sem((HALVES, FD)),
            pltpu.SemaphoreType.REGULAR,
        ],
        compiler_params=pltpu.CompilerParams(
            collective_id=0, has_side_effects=True, vmem_limit_bytes=58 * 1024 * 1024
        ),
        name="p2o_wave",
    )(
        spectrum, time_weights, interp_weights.reshape(GROUPS * BLK, BLK), group_block.reshape(1, GROUPS),
        group_count.reshape(1, 1), ws, neighbors, cp, jnp.asarray(basis), jnp.asarray(own),
    )
    new_state = state.reshape(ROWS, 2, 128).transpose(1, 0, 2).reshape(1, 2, ROWS * 128)
    return series, new_state


def solution(mesh):
    in_specs = (
        P(None, "freq", "mesh"),
        P(None, "freq"),
        P("mesh", None, None),
        P("mesh"),
        P("mesh"),
        P("freq", None, "mesh"),
        P(None, "mesh"),
        P(None, "mesh"),
    )
    out_specs = (P("freq", "mesh"), P("freq", None, "mesh"))
    return jax.shard_map(local_step, mesh=mesh, in_specs=in_specs, out_specs=out_specs, check_vma=False)
```

time: 123 us -> 44.1 us (0.36)
  Pallas kernels: 0 us -> 35.9 us
  starting transfers between devices: 35.7 us -> 0 us
  waiting for transfers between devices: 29.4 us -> 0 us
  matrix products: 18.7 us -> 0 us
  local copies, waits for them, and re-layouts: 22.1 us -> 6.7 us
  other arithmetic: 10.8 us -> 0 us
  blocking collectives: 4.43 us -> 0 us
    pallas_call x0 -> x1, Pallas kernels: none -> 35.9 us  [local_step(): pl.pallas_call(kernel, out_shape=(jax.ShapeDtypeStruct((TL, NP), F32), ja...]
    all_to_all x4 -> x0, waiting for transfers between devices: 23.6 us -> none  [the longest x1 8.39 us: moved_by_axis(): out = lax.all_to_all(out, axes[k], k, k, tiled=True)]
    all_to_all x4 -> x0, starting transfers between devices: 21.9 us -> none  [the longest x1 7.84 us: local(): lax.all_to_all(request.reshape(owners_count * capacity), 'mesh', split_ax...]
    dot_general x3 -> x0, matrix products: 18.7 us -> none  [the longest x1 15.5 us: local(): jnp.einsum('rgp,gfp->rgf', picked, interp_weights, precision=highest)]
    ppermute x4 -> x0, starting transfers between devices: 13.8 us -> none  [the longest x2 9.14 us: extended_2(): lax.ppermute(lax.slice_in_dim(block, block.shape[dim] - width, None, axis...]
    gather x4 -> x0, local copies, waits for them, and re-layouts: 12.4 us -> none  [the longest x2 10.9 us: advance(): jnp.take(extended, neighbors, axis=0)]
    ppermute x4 -> x0, waiting for transfers between devices: 5.8 us -> none  [the longest x2 5.8 us: extended_2(): lax.ppermute(lax.slice_in_dim(block, 0, width, axis=dim), axis, backward)]
    unnamed x21 -> x3, local copies, waits for them, and re-layouts: 1.56 us -> 6.7 us
  transfers between devices with their start and end apart: 8 -> 0, of which waited for: 5 -> 0; matrix products, arithmetic and copies ran while one was open for 15% -> 0% of each run, Pallas kernels for 0% -> 0%
where the time goes in v1:
time: 44.1 us; the launch traced here: 43.9 us
  Pallas kernels  35.9 us (81%)
  local copies, waits for them, and re-layouts  6.7 us (15%)
  between operations  1.29 us (3%)
    pallas_call x1, Pallas kernels, local_step(): pl.pallas_call(kernel, out_shape=(jax.ShapeDtypeStruct((TL, NP), F32), ja...  35.9 us
    unnamed x3, local copies, waits for them, and re-layouts  6.7 us

profile of v1, /device:TPU:6, one launch (start us, length us, event | category | flops | bytes accessed | tf_op | source)
XLA Modules:
  0.0 43.9 jit_solution(1252707815340976088)
XLA Ops:
  1.3 2.7 %copy.14.spec_h = f32[2,27,4096]{2,1,0:T(8,128)} copy(f32[2,27,4096]{2,0,1:T(2,128)} %param.10) | data formatting | bytes 1769472 | tf_op args[0]
  3.9 35.9 %p2o_wave.1 = (f32[54,4096]{1,0:T(8,128)}, f32[1024,128]{1,0:T(8,128)}) custom-call(f32[2,27,4096]{2,1,0:T(8,128)} %copy.14.spec_h, f32[2,54]{1,0:T(2,128)} %tw_h.1, f32[16384,128]{1,0:T(8,128)} %bitcast.19, s32[1,128]{1,0:T(1,128)} %bitcast.23, s32[1,1]{1,0:T(1,128)} %bitcast.18.gc_h, f32[1024,128]{1,0:T(8,128)} %bitcast.21, s32[4,512]{1,0:T(4,128)} %nb_h.1, ...), custom_call_target="tpu_custom_call" | custom-call | tf_op jit(solution)/shard_map/p2o_wave/pallas_call | solution.py:369
  39.8 2.2 %copy.19 = f32[54,4096]{1,0:T(8,128)} copy(f32[54,4096]{1,0:T(8,128)} %get-tuple-element.8) | data formatting | bytes 1769472
  42.0 1.9 %copy.20 = f32[1,2,65536]{2,1,0:T(2,128)} copy(f32[1,2,65536]{2,1,0:T(2,128)} %bitcast.22) | data formatting | bytes 1048576

commit v2 on v1

--- a/solution.py
+++ b/solution.py
@@ -70,7 +70,7 @@
     spec_h, tw_h, w_h, gb_h, gc_h, ws_h, nb_h, cp_h, basis_h, own_h,
     series_o, state_o,
     xs, xp, tws, twr, twf, cb, basis, r, s2, pb, ra, wsum, ag, wf, whl, oh, ws, cp, nb, gb, gc,
-    hs, hcur, hb1, hpush, hps, sb, base1, base2, ns, lh, ee,
+    hs, hcur, hb1, hpush, hps, sb, base1, base2, lh, ee,
     lsem, tw_s, tw_r, x_s, x_r, a_s, a_r, g_s, g_r, h_s, h_r, y_s, y_r, mesh_sem,
 ):
     f = lax.axis_index("freq")
@@ -107,8 +107,9 @@
     xp[KP - 8 :, :] = jnp.zeros((8, NP), F32)
     sb[ROWS:, :] = jnp.zeros((EXT - ROWS, 256), BF16)
     local[0].wait()
-    xp[0:FL, :] = xs[0]
-    xp[FL : 2 * FL, :] = xs[1]
+    for ct in range(NBLK):
+        for part in range(2):
+            xp[FL * part : FL * (part + 1), BLK * ct : BLK * (ct + 1)] = xs[pl.ds(2 * ct + part, FL, stride=2 * NBLK), :]
     local[1].wait()
     local[6].wait()
     hs[0] = ws[pl.ds(1, HALO, stride=2), :]
@@ -346,10 +347,8 @@
         if ut == 0:
             n1 = n1 + push0
             n2 = n2 + 2.0 * push0 + push1
-        ns[pl.ds(256 * ut, 128, stride=2), :] = n1
-        ns[pl.ds(256 * ut + 1, 128, stride=2), :] = n2
-    out_c = pltpu.make_async_copy(ns, state_o, lsem.at[14])
-    out_c.start()
+        state_o[pl.ds(256 * ut, 128, stride=2), :] = n1
+        state_o[pl.ds(256 * ut + 1, 128, stride=2), :] = n2
 
     for c in tw_c + x_c[0] + x_c[1] + a_c + g_c + cur_c + b1_c + [p_c] + y_c[0] + y_c[1]:
         c.wait_send()
@@ -357,25 +356,23 @@
         c.wait_recv()
     for c in own_y:
         c.wait()
-    out_c.wait()
 
 
 def local_step(spectrum, time_weights, interp_weights, group_block, group_count, wave_state, neighbors, coupling):
     basis, own = host_basis()
     ws = wave_state.reshape(2, ROWS, 128).transpose(1, 0, 2).reshape(2 * ROWS, 128)
     cp = coupling.reshape(4, ROWS, 128).transpose(1, 0, 2).reshape(4 * ROWS, 128)
-    any_spec = pl.BlockSpec(memory_space=pl.ANY)
+    hbm_spec = pl.BlockSpec(memory_space=pltpu.HBM)
+    vmem_spec = pl.BlockSpec(memory_space=pltpu.VMEM)
     sem = pltpu.SemaphoreType.DMA
+    spec = spectrum.reshape(2, FL, NBLK, BLK).transpose(1, 2, 0, 3).reshape(FL * 2 * NBLK, BLK)
     series, state = pl.pallas_call(
         kernel,
-        out_shape=(
-            jax.ShapeDtypeStruct((TL, NP), F32),
-            jax.ShapeDtypeStruct((2 * ROWS, 128), F32),
-        ),
-        in_specs=[any_spec] * 10,
-        out_specs=(any_spec, any_spec),
+        out_shape=(pltpu.VMEM((TL, NP), F32), pltpu.VMEM((2 * ROWS, 128), F32)),
+        in_specs=[hbm_spec] * 10,
+        out_specs=(vmem_spec, vmem_spec),
         scratch_shapes=[
-            pltpu.VMEM((2, FL, NP), F32),
+            pltpu.VMEM((FL * 2 * NBLK, BLK), F32),
             pltpu.VMEM((KP, NP), F32),
             pltpu.VMEM((2, TL), F32),
             pltpu.VMEM((FD, 2, TL), F32),
@@ -404,7 +401,6 @@
             pltpu.VMEM((EXT, 256), BF16),
             pltpu.VMEM((ROWS, 128), F32),
             pltpu.VMEM((ROWS, 128), F32),
-            pltpu.VMEM((2 * ROWS, 128), F32),
             pltpu.VMEM((2, 4 * GROUPS, BLK), F32),
             pltpu.VMEM((4 * GROUPS, BLK), F32),
             sem((16,)),
@@ -417,11 +413,11 @@
             pltpu.SemaphoreType.REGULAR,
         ],
         compiler_params=pltpu.CompilerParams(
-            collective_id=0, has_side_effects=True, vmem_limit_bytes=58 * 1024 * 1024
+            collective_id=0, has_side_effects=True, vmem_limit_bytes=62 * 1024 * 1024
         ),
         name="p2o_wave",
     )(
-        spectrum, time_weights, interp_weights.reshape(GROUPS * BLK, BLK), group_block.reshape(1, GROUPS),
+        spec, time_weights, interp_weights.reshape(GROUPS * BLK, BLK), group_block.reshape(1, GROUPS),
         group_count.reshape(1, 1), ws, neighbors, cp, jnp.asarray(basis), jnp.asarray(own),
     )
     new_state = state.reshape(ROWS, 2, 128).transpose(1, 0, 2).reshape(1, 2, ROWS * 128)

time: 44.1 us -> 38.6 us (0.88)
  local copies, waits for them, and re-layouts: 6.7 us -> 1.72 us
    unnamed x3 -> x2, local copies, waits for them, and re-layouts: 6.7 us -> 1.72 us
where the time goes in v2:
time: 38.6 us; the launch traced here: 38.5 us
  Pallas kernels  35.5 us (92%)
  local copies, waits for them, and re-layouts  1.72 us (4%)
  between operations  1.29 us (3%)
    pallas_call x1, Pallas kernels, local_step(): pl.pallas_call(kernel, out_shape=(pltpu.VMEM((TL, NP), F32), pltpu.VMEM((...  35.5 us
    unnamed x2, local copies, waits for them, and re-layouts  1.72 us

profile of v2, /device:TPU:6, one launch (start us, length us, event | category | flops | bytes accessed | tf_op | source)
XLA Modules:
  0.0 38.5 jit_solution(18055254268362545203)
XLA Ops:
  1.3 35.5 %p2o_wave.1 = (f32[54,4096]{1,0:T(8,128)S(1)}, f32[1024,128]{1,0:T(8,128)S(1)}) custom-call(f32[1728,128]{1,0:T(8,128)} %bitcast.27, f32[2,54]{1,0:T(2,128)} %tw_h.1, f32[16384,128]{1,0:T(8,128)} %bitcast.25, s32[1,128]{1,0:T(1,128)} %bitcast.29, s32[1,1]{1,0:T(1,128)} %bitcast.23.gc_h, f32[1024,128]{1,0:T(8,128)} %bitcast.28, s32[4,512]{1,0:T(4,128)} %nb_h.1, ...), custom_call_target="tpu_custom_call" | custom-call | tf_op jit(solution)/shard_map/p2o_wave/pallas_call | solution.py:369
  36.8 0.9 %copy.18 = f32[54,4096]{1,0:T(8,128)} copy(f32[54,4096]{1,0:T(8,128)S(1)} %get-tuple-element.6) | data formatting | bytes 1769472
  37.7 0.8 %copy.19 = f32[1,2,65536]{2,1,0:T(2,128)} copy(f32[1,2,65536]{2,1,0:T(2,128)S(1)} %bitcast.24) | data formatting | bytes 1048576

commit v3 on v2

--- a/solution.py
+++ b/solution.py
@@ -1,3 +1,4 @@
+import functools
 import math
 
 import jax
@@ -29,6 +30,7 @@
 ROWS = 512
 HALO = 32
 EXT = 640
+SLOTS = 8
 
 
 def split_bf16(x):
@@ -69,13 +71,12 @@
 def kernel(
     spec_h, tw_h, w_h, gb_h, gc_h, ws_h, nb_h, cp_h, basis_h, own_h,
     series_o, state_o,
-    xs, xp, tws, twr, twf, cb, basis, r, s2, pb, ra, wsum, ag, wf, whl, oh, ws, cp, nb, gb, gc,
+    xs, xp, tws, twr, twf, cb, basis, r, s2, pb, ra, rs, rq, pt, gs, gr, wf, whl, oh, ws, cp, nb, gb, gc,
     hs, hcur, hb1, hpush, hps, sb, base1, base2, lh, ee,
-    lsem, tw_s, tw_r, x_s, x_r, a_s, a_r, g_s, g_r, h_s, h_r, y_s, y_r, mesh_sem,
+    lsem, tw_s, tw_r, x_s, x_r, a_s, a_r, q_s, q_r, g_s, g_r, h_s, h_r, y_s, y_r, mesh_sem,
 ):
     f = lax.axis_index("freq")
     m = lax.axis_index("mesh")
-    z, x = m // 4, m % 4
 
     def fdev(d):
         return (lax.rem(f + d, FD), m)
@@ -89,18 +90,21 @@
         )
 
     bar = pltpu.get_barrier_semaphore()
-    xline = [(f, z * 4 + lax.rem(x + d, 4)) for d in range(1, 4)]
-    zline = [(f, lax.rem(z + d, 4) * 4 + x) for d in range(1, 4)]
-    first = [fdev(d) for d in range(1, FD)] + xline + zline
-    for dev in first:
-        pl.semaphore_signal(bar, inc=1, device_id=dev, device_id_type=MESH)
+
+    def tell(sem, dev):
+        pl.semaphore_signal(sem, inc=1, device_id=dev, device_id_type=MESH)
+
+    for d in range(1, FD):
+        tell(bar, fdev(d))
+    for d in range(1, MD):
+        pl.when(m + d < MD)(functools.partial(tell, bar, mdev(d)))
 
     loads = [
         (spec_h, xs), (tw_h, tws), (own_h.at[f], cb), (nb_h, nb), (gb_h, gb), (gc_h, gc),
         (ws_h, ws), (cp_h, cp), (basis_h, basis), (w_h, wf),
     ]
     local = [pltpu.make_async_copy(s, d, lsem.at[i]) for i, (s, d) in enumerate(loads)]
-    for c in local:
+    for c in local[:7]:
         c.start()
 
     twf[...] = jnp.zeros_like(twf)
@@ -115,7 +119,7 @@
     hs[0] = ws[pl.ds(1, HALO, stride=2), :]
     hs[1] = ws[pl.ds(2 * (ROWS - HALO) + 1, HALO, stride=2), :]
 
-    pl.semaphore_wait(bar, len(first))
+    pl.semaphore_wait(bar, FD - 1 + m)
 
     tw_c = [remote(tws, twr.at[f], tw_s.at[d], tw_r.at[d], fdev(d)) for d in range(1, FD)]
     for c in tw_c:
@@ -130,8 +134,10 @@
     x_c = [[x_copy(h, d) for d in range(1, FD)] for h in range(HALVES)]
     for c in x_c[0]:
         c.start()
-    for dev in xline:
-        pl.semaphore_signal(mesh_sem, inc=1, device_id=dev, device_id_type=MESH)
+    for d in range(1, MD):
+        pl.when(m >= d)(functools.partial(tell, mesh_sem, mdev(MD - d)))
+    for c in local[7:]:
+        c.start()
     own_x = [
         pltpu.make_async_copy(
             xp.at[:, pl.ds(pl.multiple_of(f * COLS + h * HC, 128), HC)],
@@ -142,6 +148,60 @@
     ]
     for c in own_x:
         c.start()
+
+    local[4].wait()
+    local[5].wait()
+    index = lax.broadcasted_iota(jnp.int32, (1, GROUPS), 1)
+    live = index < gc[0]
+    gbv = gb[...]
+    owner = jnp.where(live, lax.shift_right_logical(gbv, 5), -1).astype(F32)
+    inner = (lax.bitwise_and(gbv, NBLK - 1) + 1).astype(F32)
+    lane_i = lax.broadcasted_iota(jnp.int32, (128, 128), 1)
+    lane = lane_i.astype(F32)
+    owner_r = jnp.broadcast_to(owner, (128, 128))
+    owner_c = jnp.transpose(owner_r)
+    earlier = lane_i < lax.broadcasted_iota(jnp.int32, (128, 128), 0)
+    rank = jnp.sum(jnp.where(jnp.logical_and(owner_r == owner_c, earlier), 1.0, 0.0), axis=1, keepdims=True)
+    slot = jnp.where(owner_c >= 0.0, owner_c * SLOTS + rank, -1.0)
+    place = jnp.where(slot == lane, 1.0, 0.0)
+    asked = jnp.sum(jnp.transpose(place) * inner, axis=1, keepdims=True) - 1.0
+    rs[...] = jnp.broadcast_to(asked, (128, 128))
+    pt[...] = place.astype(BF16)
+
+    def q_copy(d):
+        to = lax.rem(m + d, MD)
+        src = rs.at[pl.ds(pl.multiple_of(to * SLOTS, 8), SLOTS)]
+        dst = rq.at[pl.ds(pl.multiple_of(m * SLOTS, 8), SLOTS)]
+        return remote(src, dst, q_s.at[d], q_r.at[d], (f, to))
+
+    q_c = [q_copy(d) for d in range(1, MD)]
+    rq[pl.ds(pl.multiple_of(m * SLOTS, 8), SLOTS), :] = rs[pl.ds(pl.multiple_of(m * SLOTS, 8), SLOTS), :]
+    up, down = mdev(1), mdev(MD - 1)
+    above, below = m < MD - 1, m > 0
+
+    def halo_pair(i, low_src, high_src, dst):
+        return [
+            (remote(low_src, dst.at[1], h_s.at[i], h_r.at[i], down), below, above),
+            (remote(high_src, dst.at[0], h_s.at[i + 1], h_r.at[i + 1], up), above, below),
+        ]
+
+    def start_all(pairs):
+        for c, sends, _ in pairs:
+            pl.when(sends)(functools.partial(c.start))
+
+    def recv_all(pairs):
+        for c, _, gets in pairs:
+            pl.when(gets)(c.wait_recv)
+
+    cur_c = halo_pair(0, hs.at[0], hs.at[1], hcur)
+
+    def enter_mesh():
+        pl.when(above)(lambda: pl.semaphore_wait(mesh_sem, MD - 1 - m))
+        for c in q_c:
+            c.start()
+        start_all(cur_c)
+
+    pl.when(m >= MD // 2)(enter_mesh)
 
     local[2].wait()
     for c in tw_c:
@@ -177,23 +237,9 @@
         c.start()
     ra[f] = pb[pl.ds(pl.multiple_of(f * 64, 8), 64), :]
 
-    pl.semaphore_wait(mesh_sem, 3)
-    up, down = mdev(1), mdev(MD - 1)
-
-    def halo_pair(i, low_src, high_src, dst):
-        return [
-            remote(low_src, dst.at[1], h_s.at[i], h_r.at[i], down),
-            remote(high_src, dst.at[0], h_s.at[i + 1], h_r.at[i + 1], up),
-        ]
-
-    cur_c = halo_pair(0, hs.at[0], hs.at[1], hcur)
-    for c in cur_c:
-        c.start()
-
     local[3].wait()
     nbv = nb[...]
     nbv = jnp.where(nbv >= ROWS + HALO, nbv, jnp.where(nbv < HALO, nbv + ROWS, nbv - HALO)).astype(F32)
-    lane = lax.broadcasted_iota(jnp.int32, (128, 128), 1).astype(F32)
     for n in range(4):
         for ut in range(4):
             col = jnp.transpose(jnp.broadcast_to(nbv[n : n + 1, 128 * ut : 128 * (ut + 1)], (128, 128)))
@@ -212,37 +258,7 @@
 
     lax.fori_loop(0, GROUPS * BLK // 512, split_w, 0)
 
-    for i in (7,):
-        local[i].wait()
-
-    def put_ext(lo_row, value):
-        hi, lo = split_bf16(value)
-        sb[lo_row : lo_row + value.shape[0], 0:128] = hi
-        sb[lo_row : lo_row + value.shape[0], 128:256] = lo
-
-    def put_halo(buf):
-        put_ext(ROWS, jnp.where(m > 0, buf[0], 0.0))
-        put_ext(ROWS + HALO, jnp.where(m < MD - 1, buf[1], 0.0))
-
-    def spread(ut, v):
-        e = dot(oh[ut], sb[...])
-        total = jnp.zeros((128, 128), F32)
-        for n in range(4):
-            c = cp[pl.ds(512 * ut + n, 128, stride=4), :]
-            total = total + c * (e[128 * n : 128 * (n + 1), 0:128] + e[128 * n : 128 * (n + 1), 128:256] - v)
-        return total
-
-    put_ext(0, ws[pl.ds(1, ROWS, stride=2), :])
-    for c in cur_c:
-        c.wait_recv()
-    put_halo(hcur)
-    for ut in range(4):
-        cur = ws[pl.ds(256 * ut + 1, 128, stride=2), :]
-        prev = ws[pl.ds(256 * ut, 128, stride=2), :]
-        base1[128 * ut : 128 * (ut + 1), :] = 2.0 * cur - prev + spread(ut, cur)
-    b1_c = halo_pair(2, base1.at[0:HALO], base1.at[ROWS - HALO : ROWS], hb1)
-    for c in b1_c:
-        c.start()
+    pl.when(m < MD // 2)(enter_mesh)
 
     local[8].wait()
 
@@ -270,70 +286,104 @@
         c.start()
         own_y.append(c)
 
+
     transform(0)
 
+    for c in q_c:
+        c.wait_recv()
+    sel = jnp.where(rq[...] == lane, 1.0, 0.0).astype(BF16)[:, 0:NBLK]
     for c in a_c:
         c.wait_recv()
     total = ra[0]
     for i in range(1, FD):
         total = total + ra[i]
-    wsum[...] = total
-    ag[m] = total
-    g_c = [remote(wsum, ag.at[m], g_s.at[d], g_r.at[d], mdev(d)) for d in range(1, MD)]
+    hi, lo = split_bf16(total)
+    for s in range(2):
+        rows = slice(NBLK * s, NBLK * (s + 1))
+        out = dot(sel, hi[rows]) + dot(sel, lo[rows])
+        for o in range(MD):
+            gs[o, SLOTS * s : SLOTS * (s + 1), :] = out[SLOTS * o : SLOTS * (o + 1)]
+
+    def g_copy(d):
+        to = lax.rem(m + d, MD)
+        return remote(gs.at[to], gr.at[m], g_s.at[d], g_r.at[d], (f, to))
+
+    g_c = [g_copy(d) for d in range(1, MD)]
     for c in g_c:
         c.start()
+    gr[m] = gs[m]
+
+    transform(1)
+
+    for i in (7,):
+        local[i].wait()
+
+    def put_ext(lo_row, value):
+        hi, lo = split_bf16(value)
+        sb[lo_row : lo_row + value.shape[0], 0:128] = hi
+        sb[lo_row : lo_row + value.shape[0], 128:256] = lo
+
+    def put_halo(buf):
+        put_ext(ROWS, jnp.where(m > 0, buf[0], 0.0))
+        put_ext(ROWS + HALO, jnp.where(m < MD - 1, buf[1], 0.0))
+
+    def spread(ut, v):
+        e = dot(oh[ut], sb[...])
+        total = jnp.zeros((128, 128), F32)
+        for n in range(4):
+            c = cp[pl.ds(512 * ut + n, 128, stride=4), :]
+            total = total + c * (e[128 * n : 128 * (n + 1), 0:128] + e[128 * n : 128 * (n + 1), 128:256] - v)
+        return total
+
+    put_ext(0, ws[pl.ds(1, ROWS, stride=2), :])
+    recv_all(cur_c)
+    put_halo(hcur)
+    for ut in range(4):
+        cur = ws[pl.ds(256 * ut + 1, 128, stride=2), :]
+        prev = ws[pl.ds(256 * ut, 128, stride=2), :]
+        base1[128 * ut : 128 * (ut + 1), :] = 2.0 * cur - prev + spread(ut, cur)
+    b1_c = halo_pair(2, base1.at[0:HALO], base1.at[ROWS - HALO : ROWS], hb1)
+    start_all(b1_c)
+
+    for c in g_c:
+        c.wait_recv()
+    for s in range(2):
+        blocks = gr[:, SLOTS * s : SLOTS * (s + 1), :].reshape(MD * SLOTS, BLK)
+        hi, lo = split_bf16(blocks)
+        ph = dot(pt[...], hi)
+        lh[0, pl.ds(2 * s, 128, stride=4), :] = ph
+        lh[1, pl.ds(2 * s, 128, stride=4), :] = ph
+        lh[0, pl.ds(2 * s + 1, 128, stride=4), :] = dot(pt[...], lo)
+        lh[1, pl.ds(2 * s + 1, 128, stride=4), :] = jnp.zeros((128, 128), F32)
+    upper = lax.broadcasted_iota(jnp.int32, (8, 128), 0) < 4
+
+    def interp(i, carry):
+        for j in range(16):
+            rows = pl.ds(pl.multiple_of(i * 128 + 8 * j, 8), 8)
+            w = whl[pl.ds(pl.multiple_of(i * 4096 + 256 * j, 256), 256), :]
+            left = jnp.concatenate([lh[0, rows, :], lh[1, rows, :]], axis=1).astype(BF16)
+            out = dot_t(left, w)
+            ee[rows, :] = jnp.where(upper, out[:, 0:128], out[:, 128:256])
+        return carry
+
+    lax.fori_loop(0, GROUPS // 32, interp, 0)
+    push0 = ee[pl.ds(0, 128, stride=4), :] + ee[pl.ds(1, 128, stride=4), :]
+    push1 = ee[pl.ds(2, 128, stride=4), :] + ee[pl.ds(3, 128, stride=4), :]
+    hps[...] = push0[0:HALO]
+    p_c = [(remote(hps, hpush, h_s.at[4], h_r.at[4], down), below, above)]
+    start_all(p_c)
 
     put_ext(0, base1[...])
-    for c in b1_c:
-        c.wait_recv()
+    recv_all(b1_c)
     put_halo(hb1)
     for ut in range(4):
         cur = ws[pl.ds(256 * ut + 1, 128, stride=2), :]
         b1 = base1[128 * ut : 128 * (ut + 1), :]
         base2[128 * ut : 128 * (ut + 1), :] = 2.0 * b1 - cur + spread(ut, b1)
 
-    transform(1)
-
-    local[4].wait()
-    local[5].wait()
-    gbv = gb[...].astype(F32)
-    index = lax.broadcasted_iota(jnp.int32, (1, 128), 1)
-    gbv = jnp.where(index < gc[...], gbv, -1.0)
-    gcol = jnp.transpose(jnp.broadcast_to(gbv, (128, 128)))
-    pick = jnp.concatenate(
-        [jnp.where(gcol == lane + float(128 * kt), 1.0, 0.0).astype(BF16) for kt in range(4)], axis=1
-    )
-    for c in g_c:
-        c.wait_recv()
-    for s in range(2):
-        blocks = ag[:, NBLK * s : NBLK * (s + 1), :].reshape(MD * NBLK, BLK)
-        hi, lo = split_bf16(blocks)
-        ph = dot(pick, hi)
-        lh[0, pl.ds(2 * s, 128, stride=4), :] = ph
-        lh[1, pl.ds(2 * s, 128, stride=4), :] = ph
-        lh[0, pl.ds(2 * s + 1, 128, stride=4), :] = dot(pick, lo)
-        lh[1, pl.ds(2 * s + 1, 128, stride=4), :] = jnp.zeros((128, 128), F32)
-    upper = lax.broadcasted_iota(jnp.int32, (8, 128), 0) < 4
-
-    def interp(i, carry):
-        for j in range(4):
-            rows = pl.ds(pl.multiple_of(i * 32 + 8 * j, 8), 8)
-            w = whl[pl.ds(pl.multiple_of(i * 1024 + 256 * j, 256), 256), :]
-            left = jnp.concatenate([lh[0, rows, :], lh[1, rows, :]], axis=1).astype(BF16)
-            out = dot_t(left, w)
-            ee[rows, :] = jnp.where(upper, out[:, 0:128], out[:, 128:256])
-        return carry
-
-    lax.fori_loop(0, GROUPS // 8, interp, 0)
-    push0 = ee[pl.ds(0, 128, stride=4), :] + ee[pl.ds(1, 128, stride=4), :]
-    push1 = ee[pl.ds(2, 128, stride=4), :] + ee[pl.ds(3, 128, stride=4), :]
-    hps[...] = push0[0:HALO]
-    p_c = remote(hps, hpush, h_s.at[4], h_r.at[4], down)
-    p_c.start()
-
     sb[ROWS : ROWS + HALO, :] = jnp.zeros((HALO, 256), BF16)
     put_ext(0, push0)
-    p_c.wait_recv()
+    recv_all(p_c)
     put_ext(ROWS + HALO, jnp.where(m < MD - 1, hpush[...], 0.0))
     for ut in range(4):
         e = dot(oh[ut, :, 0:128], sb[0:128, :]) + dot(oh[ut, :, ROWS:EXT], sb[ROWS:EXT, :])
@@ -350,8 +400,10 @@
         state_o[pl.ds(256 * ut, 128, stride=2), :] = n1
         state_o[pl.ds(256 * ut + 1, 128, stride=2), :] = n2
 
-    for c in tw_c + x_c[0] + x_c[1] + a_c + g_c + cur_c + b1_c + [p_c] + y_c[0] + y_c[1]:
+    for c in tw_c + x_c[0] + x_c[1] + a_c + q_c + g_c + y_c[0] + y_c[1]:
         c.wait_send()
+    for c, sends, _ in cur_c + b1_c + p_c:
+        pl.when(sends)(c.wait_send)
     for c in y_c[0] + y_c[1]:
         c.wait_recv()
     for c in own_y:
@@ -383,8 +435,11 @@
             pltpu.VMEM((HALVES, FD, TL, HC), F32),
             pltpu.VMEM((16 * NBLK, BLK), F32),
             pltpu.VMEM((FD, 64, BLK), F32),
-            pltpu.VMEM((64, BLK), F32),
-            pltpu.VMEM((MD, 64, BLK), F32),
+            pltpu.VMEM((MD * SLOTS, BLK), F32),
+            pltpu.VMEM((MD * SLOTS, BLK), F32),
+            pltpu.VMEM((GROUPS, MD * SLOTS), BF16),
+            pltpu.VMEM((MD, 2 * SLOTS, BLK), F32),
+            pltpu.VMEM((MD, 2 * SLOTS, BLK), F32),
             pltpu.VMEM((GROUPS * BLK, BLK), F32),
             pltpu.VMEM((GROUPS * BLK, 2 * BLK), BF16),
             pltpu.VMEM((4, 512, EXT), BF16),
@@ -392,7 +447,7 @@
             pltpu.VMEM((4 * ROWS, 128), F32),
             pltpu.VMEM((4, ROWS), jnp.int32),
             pltpu.VMEM((1, 128), jnp.int32),
-            pltpu.VMEM((1, 1), jnp.int32),
+            pltpu.SMEM((1,), jnp.int32),
             pltpu.VMEM((2, HALO, 128), F32),
             pltpu.VMEM((2, HALO, 128), F32),
             pltpu.VMEM((2, HALO, 128), F32),
@@ -408,6 +463,7 @@
             sem((HALVES, FD)), sem((HALVES, FD)),
             sem((FD,)), sem((FD,)),
             sem((MD,)), sem((MD,)),
+            sem((MD,)), sem((MD,)),
             sem((6,)), sem((6,)),
             sem((HALVES, FD)), sem((HALVES, FD)),
             pltpu.SemaphoreType.REGULAR,
@@ -418,7 +474,7 @@
         name="p2o_wave",
     )(
         spec, time_weights, interp_weights.reshape(GROUPS * BLK, BLK), group_block.reshape(1, GROUPS),
-        group_count.reshape(1, 1), ws, neighbors, cp, jnp.asarray(basis), jnp.asarray(own),
+        group_count, ws, neighbors, cp, jnp.asarray(basis), jnp.asarray(own),
     )
     new_state = state.reshape(ROWS, 2, 128).transpose(1, 0, 2).reshape(1, 2, ROWS * 128)
     return series, new_state

time: 38.6 us -> 34.8 us (0.902)
  the two profiles are of different devices: /device:TPU:6 before, /device:TPU:1 now
where the time goes in v3:
time: 34.8 us; the launch traced here: 34.6 us
  Pallas kernels  31.6 us (91%)
  local copies, waits for them, and re-layouts  1.72 us (5%)
  between operations  1.29 us (4%)
    pallas_call x1, Pallas kernels, local_step(): pl.pallas_call(kernel, out_shape=(pltpu.VMEM((TL, NP), F32), pltpu.VMEM((...  31.6 us
    unnamed x2, local copies, waits for them, and re-layouts  1.72 us

profile of v3, /device:TPU:1, one launch (start us, length us, event | category | flops | bytes accessed | tf_op | source)
XLA Modules:
  0.0 34.6 jit_solution(4323111875649035384)
XLA Ops:
  1.3 31.6 %p2o_wave.1 = (f32[54,4096]{1,0:T(8,128)S(1)}, f32[1024,128]{1,0:T(8,128)S(1)}) custom-call(f32[1728,128]{1,0:T(8,128)} %bitcast.25, f32[2,54]{1,0:T(2,128)} %tw_h.1, f32[16384,128]{1,0:T(8,128)} %bitcast.23, s32[1,128]{1,0:T(1,128)} %bitcast.27, s32[1]{0:T(128)S(6)} %copy.20.gc_h, f32[1024,128]{1,0:T(8,128)} %bitcast.26, s32[4,512]{1,0:T(4,128)} %nb_h.1, ...), custom_call_target="tpu_custom_call" | custom-call | tf_op jit(solution)/shard_map/p2o_wave/pallas_call | solution.py:421
  32.9 0.9 %copy.18 = f32[54,4096]{1,0:T(8,128)} copy(f32[54,4096]{1,0:T(8,128)S(1)} %get-tuple-element.6) | data formatting | bytes 1769472
  33.8 0.8 %copy.19 = f32[1,2,65536]{2,1,0:T(2,128)} copy(f32[1,2,65536]{2,1,0:T(2,128)S(1)} %bitcast.22) | data formatting | bytes 1048576

commit v4 on v3

--- a/solution.py
+++ b/solution.py
@@ -22,10 +22,10 @@
 KP = 56
 NP = 4096
 COLS = NP // FD
-HALVES = 2
-HC = COLS // HALVES
+CHUNKS = ((0, 256), (256, 256))
 BLK = 128
 NBLK = NP // BLK
+NHALF = NBLK // 2
 GROUPS = 128
 ROWS = 512
 HALO = 32
@@ -71,10 +71,11 @@
 def kernel(
     spec_h, tw_h, w_h, gb_h, gc_h, ws_h, nb_h, cp_h, basis_h, own_h,
     series_o, state_o,
-    xs, xp, tws, twr, twf, cb, basis, r, s2, pb, ra, rs, rq, pt, gs, gr, wf, whl, oh, ws, cp, nb, gb, gc,
+    xs, xp, tws, twr, twf, cb, basis, r0, r1, s20, s21, pb, pr, ps, ra, rs, rq, pt, gs, gr, wf, whl, oh, ws, cp, nb, gb, gc,
     hs, hcur, hb1, hpush, hps, sb, base1, base2, lh, ee,
     lsem, tw_s, tw_r, x_s, x_r, a_s, a_r, q_s, q_r, g_s, g_r, h_s, h_r, y_s, y_r, mesh_sem,
 ):
+    r, s2 = (r0, r1), (s20, s21)
     f = lax.axis_index("freq")
     m = lax.axis_index("mesh")
 
@@ -125,13 +126,16 @@
     for c in tw_c:
         c.start()
 
+    def cols_of(dev, h):
+        first, width = CHUNKS[h]
+        return pl.ds(pl.multiple_of(dev * COLS + first, 128), width)
+
     def x_copy(h, d):
         to = lax.rem(f + d, FD)
-        cols = pl.ds(pl.multiple_of(to * COLS + h * HC, 128), HC)
         rows = pl.ds(pl.multiple_of(f * KP, 8), KP)
-        return remote(xp.at[:, cols], r.at[h, rows], x_s.at[h, d], x_r.at[h, d], (to, m))
-
-    x_c = [[x_copy(h, d) for d in range(1, FD)] for h in range(HALVES)]
+        return remote(xp.at[:, cols_of(to, h)], r[h].at[rows], x_s.at[h, d], x_r.at[h, d], (to, m))
+
+    x_c = [[x_copy(h, d) for d in range(1, FD)] for h in range(len(CHUNKS))]
     for c in x_c[0]:
         c.start()
     for d in range(1, MD):
@@ -140,11 +144,9 @@
         c.start()
     own_x = [
         pltpu.make_async_copy(
-            xp.at[:, pl.ds(pl.multiple_of(f * COLS + h * HC, 128), HC)],
-            r.at[h, pl.ds(pl.multiple_of(f * KP, 8), KP)],
-            lsem.at[10 + h],
+            xp.at[:, cols_of(f, h)], r[h].at[pl.ds(pl.multiple_of(f * KP, 8), KP)], lsem.at[10 + h]
         )
-        for h in range(HALVES)
+        for h in range(len(CHUNKS))
     ]
     for c in own_x:
         c.start()
@@ -224,18 +226,25 @@
         both = dot(ghl, xh)
         part = both[0:16] + both[16:32] + dot(gh, xl)
         for b in range(4):
-            pb[pl.ds(4 * q + b, 16, stride=NBLK), :] = part[:, 128 * b : 128 * (b + 1)]
+            pb[q // 4, pl.ds(4 * (q % 4) + b, 16, stride=NHALF), :] = part[:, 128 * b : 128 * (b + 1)]
+
+    core = lax.rem(f, 2)
+    pair_c = remote(pb.at[1 - core], pr, a_s.at[0], a_r.at[0], (f + 1 - 2 * core, m))
+    pair_c.start()
+    pair_c.wait_recv()
+    ps[...] = pb[core] + pr[...]
 
     def a_copy(d):
         to = lax.rem(f + d, FD)
-        return remote(pb.at[pl.ds(pl.multiple_of(to * 64, 8), 64)], ra.at[f], a_s.at[d], a_r.at[d], (to, m))
+        src = ps.at[pl.ds(pl.multiple_of(to * 2 * NHALF, 8), 2 * NHALF)]
+        return remote(src, ra.at[f], a_s.at[d], a_r.at[d], (to, m))
 
     a_c = [a_copy(d) for d in range(1, FD)]
     for c in a_c:
         c.start()
     for c in x_c[1]:
         c.start()
-    ra[f] = pb[pl.ds(pl.multiple_of(f * 64, 8), 64), :]
+    ra[f] = ps[pl.ds(pl.multiple_of(f * 2 * NHALF, 8), 2 * NHALF), :]
 
     local[3].wait()
     nbv = nb[...]
@@ -264,24 +273,23 @@
 
     def y_copy(h, d):
         to = lax.rem(f + d, FD)
-        cols = pl.ds(pl.multiple_of(f * COLS + h * HC, 128), HC)
-        return remote(s2.at[h, to], series_o.at[:, cols], y_s.at[h, d], y_r.at[h, d], (to, m))
-
-    y_c = [[y_copy(h, d) for d in range(1, FD)] for h in range(HALVES)]
+        return remote(s2[h].at[to], series_o.at[:, cols_of(f, h)], y_s.at[h, d], y_r.at[h, d], (to, m))
+
+    y_c = [[y_copy(h, d) for d in range(1, FD)] for h in range(len(CHUNKS))]
     own_y = []
 
     def transform(h):
         for c in x_c[h]:
             c.wait_recv()
         own_x[h].wait()
-        xh, xl = split_bf16(r[h])
+        xh, xl = split_bf16(r[h][...])
         out = dot(basis[0], xh) + dot(basis[0], xl) + dot(basis[1], xh)
         for w in range(FD):
-            s2[h, w] = out[KP * w : KP * w + TL]
+            s2[h][w] = out[KP * w : KP * w + TL]
         for c in y_c[h]:
             c.start()
         c = pltpu.make_async_copy(
-            s2.at[h, f], series_o.at[:, pl.ds(pl.multiple_of(f * COLS + h * HC, 128), HC)], lsem.at[12 + h]
+            s2[h].at[f], series_o.at[:, cols_of(f, h)], lsem.at[12 + h]
         )
         c.start()
         own_y.append(c)
@@ -294,13 +302,11 @@
     sel = jnp.where(rq[...] == lane, 1.0, 0.0).astype(BF16)[:, 0:NBLK]
     for c in a_c:
         c.wait_recv()
-    total = ra[0]
-    for i in range(1, FD):
-        total = total + ra[i]
-    hi, lo = split_bf16(total)
+    total = [ra[c] + ra[2 + c] + ra[4 + c] + ra[6 + c] for c in range(2)]
     for s in range(2):
-        rows = slice(NBLK * s, NBLK * (s + 1))
-        out = dot(sel, hi[rows]) + dot(sel, lo[rows])
+        rows = slice(NHALF * s, NHALF * (s + 1))
+        hi, lo = split_bf16(jnp.concatenate([total[0][rows], total[1][rows]], axis=0))
+        out = dot(sel, hi) + dot(sel, lo)
         for o in range(MD):
             gs[o, SLOTS * s : SLOTS * (s + 1), :] = out[SLOTS * o : SLOTS * (o + 1)]
 
@@ -400,13 +406,21 @@
         state_o[pl.ds(256 * ut, 128, stride=2), :] = n1
         state_o[pl.ds(256 * ut + 1, 128, stride=2), :] = n2
 
-    for c in tw_c + x_c[0] + x_c[1] + a_c + q_c + g_c + y_c[0] + y_c[1]:
+    for c in [pair_c] + tw_c + x_c[0] + x_c[1] + a_c + q_c + g_c + y_c[0] + y_c[1]:
         c.wait_send()
     for c, sends, _ in cur_c + b1_c + p_c:
         pl.when(sends)(c.wait_send)
     for c in y_c[0] + y_c[1]:
         c.wait_recv()
     for c in own_y:
+        c.wait()
+
+
+def write_out(series, state, series_o, state_o, sem):
+    copies = [pltpu.make_async_copy(series, series_o, sem.at[0]), pltpu.make_async_copy(state, state_o, sem.at[1])]
+    for c in copies:
+        c.start()
+    for c in copies:
         c.wait()
 
 
@@ -431,10 +445,12 @@
             pltpu.VMEM((16, 128), F32),
             pltpu.VMEM((2, 64, FD * 64), BF16),
             pltpu.VMEM((2, FD * KP, FD * KP), BF16),
-            pltpu.VMEM((HALVES, FD * KP, HC), F32),
-            pltpu.VMEM((HALVES, FD, TL, HC), F32),
-            pltpu.VMEM((16 * NBLK, BLK), F32),
-            pltpu.VMEM((FD, 64, BLK), F32),
+            *[pltpu.VMEM((FD * KP, width), F32) for _, width in CHUNKS],
+            *[pltpu.VMEM((FD, TL, width), F32) for _, width in CHUNKS],
+            pltpu.VMEM((2, 16 * NHALF, BLK), F32),
+            pltpu.VMEM((16 * NHALF, BLK), F32),
+            pltpu.VMEM((16 * NHALF, BLK), F32),
+            pltpu.VMEM((FD, 2 * NHALF, BLK), F32),
             pltpu.VMEM((MD * SLOTS, BLK), F32),
             pltpu.VMEM((MD * SLOTS, BLK), F32),
             pltpu.VMEM((GROUPS, MD * SLOTS), BF16),
@@ -460,12 +476,12 @@
             pltpu.VMEM((4 * GROUPS, BLK), F32),
             sem((16,)),
             sem((FD,)), sem((FD,)),
-            sem((HALVES, FD)), sem((HALVES, FD)),
+            sem((len(CHUNKS), FD)), sem((len(CHUNKS), FD)),
             sem((FD,)), sem((FD,)),
             sem((MD,)), sem((MD,)),
             sem((MD,)), sem((MD,)),
             sem((6,)), sem((6,)),
-            sem((HALVES, FD)), sem((HALVES, FD)),
+            sem((len(CHUNKS), FD)), sem((len(CHUNKS), FD)),
             pltpu.SemaphoreType.REGULAR,
         ],
         compiler_params=pltpu.CompilerParams(
@@ -476,6 +492,14 @@
         spec, time_weights, interp_weights.reshape(GROUPS * BLK, BLK), group_block.reshape(1, GROUPS),
         group_count, ws, neighbors, cp, jnp.asarray(basis), jnp.asarray(own),
     )
+    series, state = pl.pallas_call(
+        write_out,
+        out_shape=(jax.ShapeDtypeStruct((TL, NP), F32), jax.ShapeDtypeStruct((2 * ROWS, 128), F32)),
+        in_specs=[pl.BlockSpec(memory_space=pltpu.VMEM)] * 2,
+        out_specs=(hbm_spec, hbm_spec),
+        scratch_shapes=[sem((2,))],
+        name="write_out",
+    )(pltpu.with_memory_space_constraint(series, pltpu.VMEM), pltpu.with_memory_space_constraint(state, pltpu.VMEM))
     new_state = state.reshape(ROWS, 2, 128).transpose(1, 0, 2).reshape(1, 2, ROWS * 128)
     return series, new_state
 

time: 34.8 us -> 33.2 us (0.954)
  the two profiles are of different devices: /device:TPU:1 before, /device:TPU:6 now
where the time goes in v4:
time: 33.2 us; the launch traced here: 32.9 us
  Pallas kernels  31.6 us (95%)
  between operations  1.29 us (4%)
    pallas_call x1, Pallas kernels, local_step(): pl.pallas_call(kernel, out_shape=(pltpu.VMEM((TL, NP), F32), pltpu.VMEM((...  30.5 us
    pallas_call x1, Pallas kernels, local_step(): pl.pallas_call(write_out, out_shape=(jax.ShapeDtypeStruct((TL, NP), F32),...  1.11 us

profile of v4, /device:TPU:6, one launch (start us, length us, event | category | flops | bytes accessed | tf_op | source)
XLA Modules:
  0.0 32.9 jit_solution(8159500406421187915)
XLA Ops:
  1.3 30.5 %p2o_wave.1 = (f32[54,4096]{1,0:T(8,128)S(1)}, f32[1024,128]{1,0:T(8,128)S(1)}) custom-call(f32[1728,128]{1,0:T(8,128)} %bitcast.24, f32[2,54]{1,0:T(2,128)} %tw_h.1, f32[16384,128]{1,0:T(8,128)} %bitcast.22, s32[1,128]{1,0:T(1,128)} %bitcast.26, s32[1]{0:T(128)S(6)} %copy.16.gc_h, f32[1024,128]{1,0:T(8,128)} %bitcast.25, s32[4,512]{1,0:T(4,128)} %nb_h.1, ...), custom_call_target="tpu_custom_call" | custom-call | tf_op jit(solution)/shard_map/p2o_wave/pallas_call | solution.py:435
  31.8 1.1 %write_out.1 = (f32[54,4096]{1,0:T(8,128)}, f32[1024,128]{1,0:T(8,128)}) custom-call(f32[54,4096]{1,0:T(8,128)S(1)} %get-tuple-element.6.series, f32[1024,128]{1,0:T(8,128)S(1)} %get-tuple-element.7.state), custom_call_target="tpu_custom_call" | custom-call | tf_op jit(solution)/shard_map/write_out/pallas_call | solution.py:495

commit v5 on v4

--- a/solution.py
+++ b/solution.py
@@ -22,7 +22,8 @@
 KP = 56
 NP = 4096
 COLS = NP // FD
-CHUNKS = ((0, 256), (256, 256))
+CHUNKS = ((0, 256), (256, 128), (384, 128))
+EARLY = 2
 BLK = 128
 NBLK = NP // BLK
 NHALF = NBLK // 2
@@ -71,11 +72,12 @@
 def kernel(
     spec_h, tw_h, w_h, gb_h, gc_h, ws_h, nb_h, cp_h, basis_h, own_h,
     series_o, state_o,
-    xs, xp, tws, twr, twf, cb, basis, r0, r1, s20, s21, pb, pr, ps, ra, rs, rq, pt, gs, gr, wf, whl, oh, ws, cp, nb, gb, gc,
+    xs, xp, tws, twr, twf, cb, basis, r0, r1, r2, s20, s21, s22, pb, pr, ps, ra, rs, rq, pt, gs, gr, wf, whl, oh, ws, cp, nb, gb, gc,
     hs, hcur, hb1, hpush, hps, sb, base1, base2, lh, ee,
     lsem, tw_s, tw_r, x_s, x_r, a_s, a_r, q_s, q_r, g_s, g_r, h_s, h_r, y_s, y_r, mesh_sem,
 ):
-    r, s2 = (r0, r1), (s20, s21)
+    r = (r0, r1, r2)
+    s2 = (s20, s21, s22)
     f = lax.axis_index("freq")
     m = lax.axis_index("mesh")
 
@@ -136,8 +138,9 @@
         return remote(xp.at[:, cols_of(to, h)], r[h].at[rows], x_s.at[h, d], x_r.at[h, d], (to, m))
 
     x_c = [[x_copy(h, d) for d in range(1, FD)] for h in range(len(CHUNKS))]
-    for c in x_c[0]:
-        c.start()
+    for h in range(EARLY):
+        for c in x_c[h]:
+            c.start()
     for d in range(1, MD):
         pl.when(m >= d)(functools.partial(tell, mesh_sem, mdev(MD - d)))
     for c in local[7:]:
@@ -242,8 +245,9 @@
     a_c = [a_copy(d) for d in range(1, FD)]
     for c in a_c:
         c.start()
-    for c in x_c[1]:
-        c.start()
+    for h in range(EARLY, len(CHUNKS)):
+        for c in x_c[h]:
+            c.start()
     ra[f] = ps[pl.ds(pl.multiple_of(f * 2 * NHALF, 8), 2 * NHALF), :]
 
     local[3].wait()
@@ -289,7 +293,7 @@
         for c in y_c[h]:
             c.start()
         c = pltpu.make_async_copy(
-            s2[h].at[f], series_o.at[:, cols_of(f, h)], lsem.at[12 + h]
+            s2[h].at[f], series_o.at[:, cols_of(f, h)], lsem.at[13 + h]
         )
         c.start()
         own_y.append(c)
@@ -319,8 +323,6 @@
         c.start()
     gr[m] = gs[m]
 
-    transform(1)
-
     for i in (7,):
         local[i].wait()
 
@@ -350,6 +352,17 @@
         base1[128 * ut : 128 * (ut + 1), :] = 2.0 * cur - prev + spread(ut, cur)
     b1_c = halo_pair(2, base1.at[0:HALO], base1.at[ROWS - HALO : ROWS], hb1)
     start_all(b1_c)
+
+    transform(1)
+    transform(2)
+
+    put_ext(0, base1[...])
+    recv_all(b1_c)
+    put_halo(hb1)
+    for ut in range(4):
+        cur = ws[pl.ds(256 * ut + 1, 128, stride=2), :]
+        b1 = base1[128 * ut : 128 * (ut + 1), :]
+        base2[128 * ut : 128 * (ut + 1), :] = 2.0 * b1 - cur + spread(ut, b1)
 
     for c in g_c:
         c.wait_recv()
@@ -372,20 +385,14 @@
             ee[rows, :] = jnp.where(upper, out[:, 0:128], out[:, 128:256])
         return carry
 
-    lax.fori_loop(0, GROUPS // 32, interp, 0)
+    interp(0, 0)
+    hps[...] = ee[pl.ds(0, HALO, stride=4), :] + ee[pl.ds(1, HALO, stride=4), :]
+    p_c = [(remote(hps, hpush, h_s.at[4], h_r.at[4], down), below, above)]
+    start_all(p_c)
+    for i in range(1, GROUPS // 32):
+        interp(i, 0)
     push0 = ee[pl.ds(0, 128, stride=4), :] + ee[pl.ds(1, 128, stride=4), :]
     push1 = ee[pl.ds(2, 128, stride=4), :] + ee[pl.ds(3, 128, stride=4), :]
-    hps[...] = push0[0:HALO]
-    p_c = [(remote(hps, hpush, h_s.at[4], h_r.at[4], down), below, above)]
-    start_all(p_c)
-
-    put_ext(0, base1[...])
-    recv_all(b1_c)
-    put_halo(hb1)
-    for ut in range(4):
-        cur = ws[pl.ds(256 * ut + 1, 128, stride=2), :]
-        b1 = base1[128 * ut : 128 * (ut + 1), :]
-        base2[128 * ut : 128 * (ut + 1), :] = 2.0 * b1 - cur + spread(ut, b1)
 
     sb[ROWS : ROWS + HALO, :] = jnp.zeros((HALO, 256), BF16)
     put_ext(0, push0)
@@ -406,11 +413,11 @@
         state_o[pl.ds(256 * ut, 128, stride=2), :] = n1
         state_o[pl.ds(256 * ut + 1, 128, stride=2), :] = n2
 
-    for c in [pair_c] + tw_c + x_c[0] + x_c[1] + a_c + q_c + g_c + y_c[0] + y_c[1]:
+    for c in [pair_c] + tw_c + sum(x_c, []) + a_c + q_c + g_c + sum(y_c, []):
         c.wait_send()
     for c, sends, _ in cur_c + b1_c + p_c:
         pl.when(sends)(c.wait_send)
-    for c in y_c[0] + y_c[1]:
+    for c in sum(y_c, []):
         c.wait_recv()
     for c in own_y:
         c.wait()

time: 33.2 us -> 32.9 us (level)
  no operation moved by 1% of the time
where the time goes in v5:
time: 32.9 us; the launch traced here: 32.7 us
  Pallas kernels  31.5 us (96%)
  between operations  1.29 us (4%)
    pallas_call x1, Pallas kernels, local_step(): pl.pallas_call(kernel, out_shape=(pltpu.VMEM((TL, NP), F32), pltpu.VMEM((...  30.3 us
    pallas_call x1, Pallas kernels, local_step(): pl.pallas_call(write_out, out_shape=(jax.ShapeDtypeStruct((TL, NP), F32),...  1.11 us

profile of v5, /device:TPU:6, one launch (start us, length us, event | category | flops | bytes accessed | tf_op | source)
XLA Modules:
  0.0 32.7 jit_solution(15493488238787367243)
XLA Ops:
  1.3 30.3 %p2o_wave.1 = (f32[54,4096]{1,0:T(8,128)S(1)}, f32[1024,128]{1,0:T(8,128)S(1)}) custom-call(f32[1728,128]{1,0:T(8,128)} %bitcast.24, f32[2,54]{1,0:T(2,128)} %tw_h.1, f32[16384,128]{1,0:T(8,128)} %bitcast.22, s32[1,128]{1,0:T(1,128)} %bitcast.26, s32[1]{0:T(128)S(6)} %copy.16.gc_h, f32[1024,128]{1,0:T(8,128)} %bitcast.25, s32[4,512]{1,0:T(4,128)} %nb_h.1, ...), custom_call_target="tpu_custom_call" | custom-call | tf_op jit(solution)/shard_map/p2o_wave/pallas_call | solution.py:442
  31.6 1.1 %write_out.1 = (f32[54,4096]{1,0:T(8,128)}, f32[1024,128]{1,0:T(8,128)}) custom-call(f32[54,4096]{1,0:T(8,128)S(1)} %get-tuple-element.6.series, f32[1024,128]{1,0:T(8,128)S(1)} %get-tuple-element.7.state), custom_call_target="tpu_custom_call" | custom-call | tf_op jit(solution)/shard_map/write_out/pallas_call | solution.py:502

commit v6 on v5

--- a/solution.py
+++ b/solution.py
@@ -103,7 +103,7 @@
         pl.when(m + d < MD)(functools.partial(tell, bar, mdev(d)))
 
     loads = [
-        (spec_h, xs), (tw_h, tws), (own_h.at[f], cb), (nb_h, nb), (gb_h, gb), (gc_h, gc),
+        (spec_h, xs.at[0 : FL * 2 * NBLK]), (tw_h, tws), (own_h.at[f], cb), (nb_h, nb), (gb_h, gb), (gc_h, gc),
         (ws_h, ws), (cp_h, cp), (basis_h, basis), (w_h, wf),
     ]
     local = [pltpu.make_async_copy(s, d, lsem.at[i]) for i, (s, d) in enumerate(loads)]
@@ -445,7 +445,7 @@
         in_specs=[hbm_spec] * 10,
         out_specs=(vmem_spec, vmem_spec),
         scratch_shapes=[
-            pltpu.VMEM((FL * 2 * NBLK, BLK), F32),
+            pltpu.VMEM((32 * 2 * NBLK, BLK), F32),
             pltpu.VMEM((KP, NP), F32),
             pltpu.VMEM((2, TL), F32),
             pltpu.VMEM((FD, 2, TL), F32),

time: 32.9 us -> 32.9 us (level)
  no operation moved by 1% of the time
where the time goes in v6:
time: 32.9 us; the launch traced here: 32.7 us
  Pallas kernels  31.5 us (96%)
  between operations  1.29 us (4%)
    pallas_call x1, Pallas kernels, local_step(): pl.pallas_call(kernel, out_shape=(pltpu.VMEM((TL, NP), F32), pltpu.VMEM((...  30.3 us
    pallas_call x1, Pallas kernels, local_step(): pl.pallas_call(write_out, out_shape=(jax.ShapeDtypeStruct((TL, NP), F32),...  1.11 us

profile of v6, /device:TPU:6, one launch (start us, length us, event | category | flops | bytes accessed | tf_op | source)
XLA Modules:
  0.0 32.7 jit_solution(3894069981028405038)
XLA Ops:
  1.3 30.3 %p2o_wave.1 = (f32[54,4096]{1,0:T(8,128)S(1)}, f32[1024,128]{1,0:T(8,128)S(1)}) custom-call(f32[1728,128]{1,0:T(8,128)} %bitcast.24, f32[2,54]{1,0:T(2,128)} %tw_h.1, f32[16384,128]{1,0:T(8,128)} %bitcast.22, s32[1,128]{1,0:T(1,128)} %bitcast.26, s32[1]{0:T(128)S(6)} %copy.16.gc_h, f32[1024,128]{1,0:T(8,128)} %bitcast.25, s32[4,512]{1,0:T(4,128)} %nb_h.1, ...), custom_call_target="tpu_custom_call" | custom-call | tf_op jit(solution)/shard_map/p2o_wave/pallas_call | solution.py:442
  31.6 1.1 %write_out.1 = (f32[54,4096]{1,0:T(8,128)}, f32[1024,128]{1,0:T(8,128)}) custom-call(f32[54,4096]{1,0:T(8,128)S(1)} %get-tuple-element.6.series, f32[1024,128]{1,0:T(8,128)S(1)} %get-tuple-element.7.state), custom_call_target="tpu_custom_call" | custom-call | tf_op jit(solution)/shard_map/write_out/pallas_call | solution.py:502
